TPU v7x, 128 devices: a whole 4x4x4 slice. The times are simulated.
128 devices in a mesh: tile: 32 (over x, z, core), dir: 4 (over y).
Axes of the slice: x: 4, y: 4, z: 4, core: 2. Of those that a mesh axis runs over, the one named last changes fastest.
Arguments:
- probes: float32 [32, 256, 32, 128], P('dir', 'tile'), may hold values from -6 to 6
- base_sens: float32 [256, 32, 128], P('tile'), may hold values from -12 to 12
- obs_weight: float32 [256, 32, 128], P('tile'), may hold values from 1 to 10
- perm: float32 [256, 32, 128], P('tile'), may hold values from 0.25 to 4
- material: int32 [256, 32, 128], P('tile'), may hold values from 0 to 7
- class_storage: float32 [8], replicated, may hold values from 0.2 to 2
- class_alpha: float32 [8], replicated, may hold values from 0.5 to 1
- class_bulk: float32 [8], replicated, may hold values from 0.25 to 2
- class_shear: float32 [8], replicated, may hold values from 0.5 to 4
Outputs:
- hess_block: float32 [32, 256, 32, 128], P('dir', 'tile')
- r_factor: float32 [32, 32], replicated
All inputs are finite; a program needn't handle non-finite values.
Results may differ from a plain program's by a relative error of at most 0.00016.
Values sent between devices are 32-bit elements; how exact they have to be, the bound alone decides.
A program may use at most 64 MiB of HBM per device.

v0:
```python
import jax
import jax.numpy as jnp
from jax import lax
from jax.sharding import Mesh
from jax.sharding import PartitionSpec as P

NCLASS = 8
SWEEPS = 2
STEPS = 2
TILE = ("tile_0", "tile_1", "tile_2")
TILE_DIR = ("tile_0", "tile_1", "tile_2", "dir")


def copy_for_each(value, axis):
    peers = lax.axis_size(axis)
    return lax.all_to_all(
        jnp.broadcast_to(value[None], (peers, *value.shape)), axis, 0, 0, tiled=True
    )


def taken_together(value, axis):
    return copy_for_each(value, axis).sum(axis=0)


def extended(cells, sides, width):
    for axis, dim in sides:
        count = lax.axis_size(axis)
        ends = count - 1
        head = lax.slice_in_dim(cells, 0, width, axis=dim)
        tail = lax.slice_in_dim(cells, cells.shape[dim] - width, cells.shape[dim], axis=dim)
        cells = jnp.concatenate(
            [
                lax.ppermute(tail, axis, [(i, (i + 1) % count) for i in range(ends)]),
                cells,
                lax.ppermute(head, axis, [((i + 1) % count, i) for i in range(ends)]),
            ],
            axis=dim,
        )
    return cells


def over_axes(value, axes):
    for axis in axes:
        value = lax.psum(value, axis)
    return value


def pad_second(field):
    return jnp.pad(field, [(0, 0)] * (field.ndim - 2) + [(1, 1), (0, 0)])


def pad_third(field):
    return jnp.pad(field, [(0, 0)] * (field.ndim - 1) + [(1, 1)])


def face_flux(padded, coef_pad):
    center = padded[..., 1:-1, :, :]
    coef_mid = coef_pad[1:-1]
    result = 0.5 * (coef_mid + coef_pad[2:]) * (center - padded[..., 2:, :, :])
    result = result + 0.5 * (coef_mid + coef_pad[:-2]) * (center - padded[..., :-2, :, :])
    field_y = pad_second(center)
    coef_y = pad_second(coef_mid)
    result = result + 0.5 * (coef_mid + coef_y[:, 2:]) * (center - field_y[..., 2:, :])
    result = result + 0.5 * (coef_mid + coef_y[:, :-2]) * (center - field_y[..., :-2, :])
    field_z = pad_third(center)
    coef_z = pad_third(coef_mid)
    result = result + 0.5 * (coef_mid + coef_z[:, :, 2:]) * (center - field_z[..., 2:])
    result = result + 0.5 * (coef_mid + coef_z[:, :, :-2]) * (center - field_z[..., :-2])
    return result


def gradient(press_pad, biot):
    first = 0.5 * biot * (press_pad[..., 2:, :, :] - press_pad[..., :-2, :, :])
    center = press_pad[..., 1:-1, :, :]
    field_y = pad_second(center)
    second = 0.5 * biot * (field_y[..., 2:, :] - field_y[..., :-2, :])
    field_z = pad_third(center)
    third = 0.5 * biot * (field_z[..., 2:] - field_z[..., :-2])
    return jnp.stack([first, second, third])


def divergence(first_pad, others, biot_pad):
    weighted = biot_pad * first_pad
    result = 0.5 * (weighted[..., :-2, :, :] - weighted[..., 2:, :, :])
    biot = biot_pad[1:-1]
    second = pad_second(biot * others[0])
    result = result + 0.5 * (second[..., :-2, :] - second[..., 2:, :])
    third = pad_third(biot * others[1])
    result = result + 0.5 * (third[..., :-2] - third[..., 2:])
    return result


def inner(left, right):
    summed = jnp.sum(left * right, axis=(-3, -2, -1))
    if summed.ndim == 2:
        summed = jnp.sum(summed, axis=0)
    return taken_together(summed, TILE)


def spread(values):
    return values[:, None, None, None]


def pad_scalar(field):
    return extended(field, ((TILE, 1),), 1)


def pad_vector(field):
    return extended(field, ((TILE, 2),), 1)


def conj_grad(operate, extend, target, iterate, iter_pad):
    if iterate is None:
        residual = target
        iterate = jnp.zeros_like(target)
    else:
        residual = target - operate(iter_pad)
    direction = residual
    norm_now = inner(residual, residual)
    for step in range(STEPS):
        image = operate(extend(direction))
        step_len = norm_now / inner(direction, image)
        iterate = iterate + spread(step_len) * direction
        if step + 1 < STEPS:
            residual = residual - spread(step_len) * image
            norm_next = inner(residual, residual)
            direction = residual + spread(norm_next / norm_now) * direction
            norm_now = norm_next
    return iterate


def body(
    probes,
    base_sens,
    obs_weight,
    perm,
    material,
    class_storage,
    class_alpha,
    class_bulk,
    class_shear,
):
    class_mask = (
        material[None] == jnp.arange(NCLASS, dtype=jnp.int32)[:, None, None, None]
    ).astype(jnp.float32)
    storage = jnp.sum(class_storage[:, None, None, None] * class_mask, axis=0)
    biot = jnp.sum(class_alpha[:, None, None, None] * class_mask, axis=0)
    bulk = jnp.sum(class_bulk[:, None, None, None] * class_mask, axis=0)
    shear = jnp.sum(class_shear[:, None, None, None] * class_mask, axis=0)
    stab_term = biot * biot / bulk
    diagonal = storage + stab_term
    coef_all = extended(jnp.stack([perm, biot, shear]), ((TILE, 1),), 1)
    perm_pad = coef_all[0]
    biot_pad = coef_all[1]
    shear_pad = coef_all[2]

    def press_apply(padded):
        return diagonal * padded[..., 1:-1, :, :] + face_flux(padded, perm_pad)

    def elast_apply(padded):
        return face_flux(padded, shear_pad)

    def solve(source, orient):
        pressure = None
        displace = None
        press_pad = None
        for sweep in range(SWEEPS):
            source_term = source
            press_init = None
            disp_pad = None
            if displace is not None:
                first_pad = pad_scalar(displace[0])
                press_init = pad_scalar(pressure)
                source_term = (
                    source
                    - orient * divergence(first_pad, (displace[1], displace[2]), biot_pad)
                    + stab_term * pressure
                )
            pressure = conj_grad(press_apply, pad_scalar, source_term, pressure, press_init)
            press_pad = pad_scalar(pressure)
            elastic_term = orient * gradient(press_pad, biot)
            if displace is not None and disp_pad is None:
                disp_pad = pad_vector(displace)
            displace = conj_grad(elast_apply, pad_vector, elastic_term, displace, disp_pad)
        return pressure

    tangent = solve(base_sens * probes, 1.0)
    adjoint = solve(obs_weight * tangent, -1.0)
    hess_block = base_sens * adjoint
    cell_count = (
        hess_block.shape[1] * lax.axis_size(TILE) * hess_block.shape[2] * hess_block.shape[3]
    )
    regrouped = lax.all_to_all(hess_block, "dir", split_axis=2, concat_axis=0, tiled=True)
    columns = regrouped.reshape(regrouped.shape[0], -1)
    gram_local = (
        jnp.dot(
            columns, columns.T, precision=lax.Precision.HIGHEST, preferred_element_type=jnp.float32
        )
        / cell_count
    )
    gram_whole = over_axes(gram_local, TILE_DIR)
    r_factor = jnp.linalg.cholesky(gram_whole).T
    return (hess_block, r_factor)


def solution(mesh):
    torus = Mesh(
        mesh.devices.reshape(4, 4, 2, mesh.shape["dir"]), ("tile_0", "tile_1", "tile_2", "dir")
    )
    return jax.shard_map(
        body,
        mesh=torus,
        in_specs=(
            P("dir", TILE, None, None),
            P(TILE, None, None),
            P(TILE, None, None),
            P(TILE, None, None),
            P(TILE, None, None),
            P(),
            P(),
            P(),
            P(),
        ),
        out_specs=(P("dir", TILE, None, None), P()),
        check_vma=False,
    )
```

profile of v0, /device:TPU:0, one launch (start us, length us, event | category | flops | bytes accessed | tf_op | source)
XLA Modules:
  0.0 630.6 jit_solution(4147573573730072750)
XLA Ops:
  17.0 22.2 %all_to_all.159 = f32[32,1,8]{2,1,0:T(1,128)} all-to-all(f32[32,1,8]{2,1,0:T(1,128)S(1)} %broadcast_in_dim.50), channel_id=1, replica_groups=mesh['tile_0'=4,'tile_1'=4,'tile_2'=2,'dir'=4] {'tile_0','tile_1','tile_2'}, dimensions={0} | all-to-all | bytes 2048 | tf_op jit(solution)/shard_map/all_to_all | solution.py:16
  45.0 6.0 all-to-all-done
  52.8 10.7 %all_to_all.160 = f32[32,1,8]{2,1,0:T(1,128)S(1)} all-to-all(f32[32,1,8]{2,1,0:T(1,128)S(1)} %broadcast_in_dim.51), channel_id=1, replica_groups=mesh['tile_0'=4,'tile_1'=4,'tile_2'=2,'dir'=4] {'tile_0','tile_1','tile_2'}, dimensions={0} | all-to-all | bytes 2048 | tf_op jit(solution)/shard_map/all_to_all | solution.py:16
  72.8 16.6 %all_to_all.161 = f32[32,1,8]{2,1,0:T(1,128)S(1)} all-to-all(f32[32,1,8]{2,1,0:T(1,128)S(1)} %broadcast_in_dim.52), channel_id=1, replica_groups=mesh['tile_0'=4,'tile_1'=4,'tile_2'=2,'dir'=4] {'tile_0','tile_1','tile_2'}, dimensions={0} | all-to-all | bytes 2048 | tf_op jit(solution)/shard_map/all_to_all | solution.py:16
  109.5 22.6 %all_to_all.162 = f32[32,1,8]{2,1,0:T(1,128)} all-to-all(f32[32,1,8]{2,1,0:T(1,128)S(1)} %broadcast_in_dim.54), channel_id=1, replica_groups=mesh['tile_0'=4,'tile_1'=4,'tile_2'=2,'dir'=4] {'tile_0','tile_1','tile_2'}, dimensions={0} | all-to-all | bytes 2048 | tf_op jit(solution)/shard_map/all_to_all | solution.py:16
  137.9 6.0 all-to-all-done.4
  147.7 11.2 %all_to_all.163 = f32[32,1,8]{2,1,0:T(1,128)S(1)} all-to-all(f32[32,1,8]{2,1,0:T(1,128)S(1)} %broadcast_in_dim.55), channel_id=1, replica_groups=mesh['tile_0'=4,'tile_1'=4,'tile_2'=2,'dir'=4] {'tile_0','tile_1','tile_2'}, dimensions={0} | all-to-all | bytes 2048 | tf_op jit(solution)/shard_map/all_to_all | solution.py:16
  172.9 11.9 %all-to-all-start.7 = ((f32[32,1,8]{2,1,0:T(1,128)}), f32[32,1,8]{2,1,0:T(1,128)S(1)}, u32[]{:S(2)}, u32[]{:S(2)}) async-start(f32[32,1,8]{2,1,0:T(1,128)} %broadcast_in_dim.56), calls=%async_computation.7 | async-start | bytes 32768 | tf_op jit(solution)/shard_map/all_to_all | solution.py:16
  186.4 5.7 all-to-all-done.7
  205.8 6.1 collective-permute-start.15
  214.9 20.9 %all_to_all.164 = f32[32,1,8]{2,1,0:T(1,128)S(1)} all-to-all(f32[32,1,8]{2,1,0:T(1,128)S(1)} %broadcast_in_dim.58), channel_id=1, replica_groups=mesh['tile_0'=4,'tile_1'=4,'tile_2'=2,'dir'=4] {'tile_0','tile_1','tile_2'}, dimensions={0} | all-to-all | bytes 2048 | tf_op jit(solution)/shard_map/all_to_all | solution.py:16
  240.3 7.3 %all-to-all-done.8 = f32[32,1,8]{2,1,0:T(1,128)S(1)} async-done(((f32[32,1,8]{2,1,0:T(1,128)}), f32[32,1,8]{2,1,0:T(1,128)S(1)}, u32[]{:S(2)}, u32[]{:S(2)}) %all-to-all-start.8) | async-done | bytes 1056 | tf_op jit(solution)/shard_map/all_to_all | solution.py:16
  249.2 10.7 %all_to_all.165 = f32[32,1,8]{2,1,0:T(1,128)S(1)} all-to-all(f32[32,1,8]{2,1,0:T(1,128)S(1)} %broadcast_in_dim.59), channel_id=1, replica_groups=mesh['tile_0'=4,'tile_1'=4,'tile_2'=2,'dir'=4] {'tile_0','tile_1','tile_2'}, dimensions={0} | all-to-all | bytes 2048 | tf_op jit(solution)/shard_map/all_to_all | solution.py:16
  267.9 16.6 %all_to_all.166 = f32[32,1,8]{2,1,0:T(1,128)S(1)} all-to-all(f32[32,1,8]{2,1,0:T(1,128)S(1)} %broadcast_in_dim.60), channel_id=1, replica_groups=mesh['tile_0'=4,'tile_1'=4,'tile_2'=2,'dir'=4] {'tile_0','tile_1','tile_2'}, dimensions={0} | all-to-all | bytes 2048 | tf_op jit(solution)/shard_map/all_to_all | solution.py:16
  294.0 16.8 %all_to_all.167 = f32[32,1,8]{2,1,0:T(1,128)S(1)} all-to-all(f32[32,1,8]{2,1,0:T(1,128)S(1)} %broadcast_in_dim.62), channel_id=1, replica_groups=mesh['tile_0'=4,'tile_1'=4,'tile_2'=2,'dir'=4] {'tile_0','tile_1','tile_2'}, dimensions={0} | all-to-all | bytes 2048 | tf_op jit(solution)/shard_map/all_to_all | solution.py:16
  315.2 7.3 %all-to-all-done.12 = f32[32,1,8]{2,1,0:T(1,128)S(1)} async-done(((f32[32,1,8]{2,1,0:T(1,128)}), f32[32,1,8]{2,1,0:T(1,128)S(1)}, u32[]{:S(2)}, u32[]{:S(2)}) %all-to-all-start.12) | async-done | bytes 1056 | tf_op jit(solution)/shard_map/all_to_all | solution.py:16
  322.9 10.7 %all_to_all.168 = f32[32,1,8]{2,1,0:T(1,128)S(1)} all-to-all(f32[32,1,8]{2,1,0:T(1,128)S(1)} %broadcast_in_dim.63), channel_id=1, replica_groups=mesh['tile_0'=4,'tile_1'=4,'tile_2'=2,'dir'=4] {'tile_0','tile_1','tile_2'}, dimensions={0} | all-to-all | bytes 2048 | tf_op jit(solution)/shard_map/all_to_all | solution.py:16
  341.8 16.6 %all_to_all.169 = f32[32,1,8]{2,1,0:T(1,128)S(1)} all-to-all(f32[32,1,8]{2,1,0:T(1,128)S(1)} %broadcast_in_dim.64), channel_id=1, replica_groups=mesh['tile_0'=4,'tile_1'=4,'tile_2'=2,'dir'=4] {'tile_0','tile_1','tile_2'}, dimensions={0} | all-to-all | bytes 2048 | tf_op jit(solution)/shard_map/all_to_all | solution.py:16
  367.2 4.6 collective-permute-start.25
  377.8 22.5 %all_to_all.170 = f32[32,1,8]{2,1,0:T(1,128)} all-to-all(f32[32,1,8]{2,1,0:T(1,128)S(1)} %broadcast_in_dim.66), channel_id=1, replica_groups=mesh['tile_0'=4,'tile_1'=4,'tile_2'=2,'dir'=4] {'tile_0','tile_1','tile_2'}, dimensions={0} | all-to-all | bytes 2048 | tf_op jit(solution)/shard_map/all_to_all | solution.py:16
  406.1 6.0 all-to-all-done.16
  416.5 10.7 %all_to_all.171 = f32[32,1,8]{2,1,0:T(1,128)S(1)} all-to-all(f32[32,1,8]{2,1,0:T(1,128)S(1)} %broadcast_in_dim.67), channel_id=1, replica_groups=mesh['tile_0'=4,'tile_1'=4,'tile_2'=2,'dir'=4] {'tile_0','tile_1','tile_2'}, dimensions={0} | all-to-all | bytes 2048 | tf_op jit(solution)/shard_map/all_to_all | solution.py:16
  440.6 19.1 %all_to_all.172 = f32[32,1,8]{2,1,0:T(1,128)S(1)} all-to-all(f32[32,1,8]{2,1,0:T(1,128)S(1)} %broadcast_in_dim.68), channel_id=1, replica_groups=mesh['tile_0'=4,'tile_1'=4,'tile_2'=2,'dir'=4] {'tile_0','tile_1','tile_2'}, dimensions={0} | all-to-all | bytes 2048 | tf_op jit(solution)/shard_map/all_to_all | solution.py:16
  473.2 6.1 collective-permute-start.31
  482.3 20.9 %all_to_all.173 = f32[32,1,8]{2,1,0:T(1,128)S(1)} all-to-all(f32[32,1,8]{2,1,0:T(1,128)S(1)} %broadcast_in_dim.70), channel_id=1, replica_groups=mesh['tile_0'=4,'tile_1'=4,'tile_2'=2,'dir'=4] {'tile_0','tile_1','tile_2'}, dimensions={0} | all-to-all | bytes 2048 | tf_op jit(solution)/shard_map/all_to_all | solution.py:16
  507.7 7.3 %all-to-all-done.20 = f32[32,1,8]{2,1,0:T(1,128)S(1)} async-done(((f32[32,1,8]{2,1,0:T(1,128)}), f32[32,1,8]{2,1,0:T(1,128)S(1)}, u32[]{:S(2)}, u32[]{:S(2)}) %all-to-all-start.20) | async-done | bytes 1056 | tf_op jit(solution)/shard_map/all_to_all | solution.py:16
  516.6 10.8 %all_to_all.174 = f32[32,1,8]{2,1,0:T(1,128)S(1)} all-to-all(f32[32,1,8]{2,1,0:T(1,128)S(1)} %broadcast_in_dim.71), channel_id=1, replica_groups=mesh['tile_0'=4,'tile_1'=4,'tile_2'=2,'dir'=4] {'tile_0','tile_1','tile_2'}, dimensions={0} | all-to-all | bytes 2048 | tf_op jit(solution)/shard_map/all_to_all | solution.py:16
  535.5 16.6 %all_to_all.175 = f32[32,1,8]{2,1,0:T(1,128)S(1)} all-to-all(f32[32,1,8]{2,1,0:T(1,128)S(1)} %broadcast_in_dim.72), channel_id=1, replica_groups=mesh['tile_0'=4,'tile_1'=4,'tile_2'=2,'dir'=4] {'tile_0','tile_1','tile_2'}, dimensions={0} | all-to-all | bytes 2048 | tf_op jit(solution)/shard_map/all_to_all | solution.py:16
  554.5 19.6 %all_to_all.176 = f32[8,8,32,128]{3,1,0,2:T(8,128)S(1)} all-to-all(f32[8,8,32,128]{3,1,0,2:T(8,128)S(1)} %copy.77), channel_id=1, replica_groups=mesh['tile_0'=4,'tile_1'=4,'tile_2'=2,'dir'=4] {'dir'}, dimensions={2} | all-to-all | bytes 2097152 | tf_op jit(solution)/shard_map/all_to_all | solution.py:193
  575.9 15.3 %psum.28 = f32[32,32]{0,1:T(8,128)S(1)} all-reduce(f32[32,32]{0,1:T(8,128)S(1)} %convolution_multiply_fusion), channel_id=1, replica_groups=mesh['tile_0'=4,'tile_1'=4,'tile_2'=2,'dir'=4] {'tile_0'}, use_global_device_ids=true, to_apply=%region_52.53 | all-reduce | flops 1024 | bytes 8192 | tf_op jit(solution)/shard_map/psum | solution.py:44
  591.2 15.3 %psum.29 = f32[32,32]{0,1:T(8,128)S(1)} all-reduce(f32[32,32]{0,1:T(8,128)S(1)} %psum.28), channel_id=1, replica_groups=mesh['tile_0'=4,'tile_1'=4,'tile_2'=2,'dir'=4] {'tile_1'}, use_global_device_ids=true, to_apply=%region_53.54 | all-reduce | flops 1024 | bytes 8192 | tf_op jit(solution)/shard_map/psum | solution.py:44
  609.8 15.3 %psum.31 = f32[32,32]{0,1:T(8,128)S(1)} all-reduce(f32[32,32]{0,1:T(8,128)S(1)} %psum.30), channel_id=1, replica_groups=mesh['tile_0'=4,'tile_1'=4,'tile_2'=2,'dir'=4] {'dir'}, use_global_device_ids=true, to_apply=%region_55.56 | all-reduce | flops 1024 | bytes 8192 | tf_op jit(solution)/shard_map/psum | solution.py:44
  (396 shorter events, 211.6 us)
Async XLA Ops:
  2.9 12.2 %collective-permute-start = (f32[3,1,32,128]{3,2,1,0:T(8,128)S(1)}, f32[3,1,32,128]{3,2,1,0:T(8,128)S(1)}, u32[]{:S(2)}, u32[]{:S(2)}) collective-permute-start(f32[3,1,32,128]{3,2,1,0:T(8,128)S(1)} %get-tuple-element.86), channel_id=1, source_target_pairs={{4,0},{8,4},{12,8},{16,12},{20,16},{24,20},{28,24},{32,28},{36,32}... | collective-permute-start | bytes 147464 | tf_op jit(solution)/shard_map/ppermute | solution.py:35
  4.2 10.9 %collective-permute-start.2 = (f32[3,1,32,128]{3,2,1,0:T(8,128)S(1)}, f32[3,1,32,128]{3,2,1,0:T(8,128)S(1)}, u32[]{:S(2)}, u32[]{:S(2)}) collective-permute-start(f32[3,1,32,128]{3,2,1,0:T(8,128)S(1)} %get-tuple-element.87), channel_id=1, source_target_pairs={{0,4},{4,8},{8,12},{12,16},{16,20},{20,24},{24,28},{28,32},{32,36}... | collective-permute-start | bytes 147464 | tf_op jit(solution)/shard_map/ppermute | solution.py:33
  8.6 6.5 %collective-permute-start.1 = (f32[8,1,32,128]{3,2,1,0:T(8,128)S(1)}, f32[8,1,32,128]{3,2,1,0:T(8,128)S(1)}, u32[]{:S(2)}, u32[]{:S(2)}) collective-permute-start(f32[8,1,32,128]{3,2,1,0:T(8,128)S(1)} %get-tuple-element.80), channel_id=1, source_target_pairs={{4,0},{8,4},{12,8},{16,12},{20,16},{24,20},{28,24},{32,28},{36,32}... | collective-permute-start | bytes 393224 | tf_op jit(solution)/shard_map/ppermute | solution.py:35
  10.0 5.2 collective-permute-start.3
  39.8 11.2 %all-to-all-start = ((f32[32,1,8]{2,1,0:T(1,128)}), f32[32,1,8]{2,1,0:T(1,128)S(1)}, u32[]{:S(2)}, u32[]{:S(2)}) async-start(f32[32,1,8]{2,1,0:T(1,128)} %broadcast_in_dim.49), calls=%async_computation | async-start | bytes 32768 | tf_op jit(solution)/shard_map/all_to_all | solution.py:16
  66.4 4.3 collective-permute-start.4
  67.7 4.0 collective-permute-start.5
  89.9 4.3 collective-permute-start.6
  91.2 4.0 collective-permute-start.7
  97.7 6.2 collective-permute-start.8
  99.0 5.9 collective-permute-start.9
  132.8 11.2 %all-to-all-start.4 = ((f32[32,1,8]{2,1,0:T(1,128)}), f32[32,1,8]{2,1,0:T(1,128)S(1)}, u32[]{:S(2)}, u32[]{:S(2)}) async-start(f32[32,1,8]{2,1,0:T(1,128)} %broadcast_in_dim.53), calls=%async_computation.4 | async-start | bytes 32768 | tf_op jit(solution)/shard_map/all_to_all | solution.py:16
  163.0 4.4 collective-permute-start.10
  164.3 4.4 collective-permute-start.11
  172.9 19.3 %all-to-all-start.7 = ((f32[32,1,8]{2,1,0:T(1,128)}), f32[32,1,8]{2,1,0:T(1,128)S(1)}, u32[]{:S(2)}, u32[]{:S(2)}) async-start(f32[32,1,8]{2,1,0:T(1,128)} %broadcast_in_dim.56), calls=%async_computation.7 | async-start | bytes 32768 | tf_op jit(solution)/shard_map/all_to_all | solution.py:16
  204.5 7.4 %collective-permute-start.14 = (f32[8,1,32,128]{3,2,1,0:T(8,128)S(1)}, f32[8,1,32,128]{3,2,1,0:T(8,128)S(1)}, u32[]{:S(2)}, u32[]{:S(2)}) collective-permute-start(f32[8,1,32,128]{3,2,1,0:T(8,128)S(1)} %get-tuple-element.72), channel_id=1, source_target_pairs={{4,0},{8,4},{12,8},{16,12},{20,16},{24,20},{28,24},{32,28},{36,32}... | collective-permute-start | bytes 393224 | tf_op jit(solution)/shard_map/ppermute | solution.py:35
  205.8 7.1 %collective-permute-start.15 = (f32[8,1,32,128]{3,2,1,0:T(8,128)S(1)}, f32[8,1,32,128]{3,2,1,0:T(8,128)S(1)}, u32[]{:S(2)}, u32[]{:S(2)}) collective-permute-start(f32[8,1,32,128]{3,2,1,0:T(8,128)S(1)} %get-tuple-element.73), channel_id=1, source_target_pairs={{0,4},{4,8},{8,12},{12,16},{16,20},{20,24},{24,28},{28,32},{32,36}... | collective-permute-start | bytes 393224 | tf_op jit(solution)/shard_map/ppermute | solution.py:33
  236.4 11.2 %all-to-all-start.8 = ((f32[32,1,8]{2,1,0:T(1,128)}), f32[32,1,8]{2,1,0:T(1,128)S(1)}, u32[]{:S(2)}, u32[]{:S(2)}) async-start(f32[32,1,8]{2,1,0:T(1,128)} %broadcast_in_dim.57), calls=%async_computation.8 | async-start | bytes 32768 | tf_op jit(solution)/shard_map/all_to_all | solution.py:16
  261.5 4.3 collective-permute-start.16
  286.3 4.5 collective-permute-start.18
  311.3 11.2 %all-to-all-start.12 = ((f32[32,1,8]{2,1,0:T(1,128)}), f32[32,1,8]{2,1,0:T(1,128)S(1)}, u32[]{:S(2)}, u32[]{:S(2)}) async-start(f32[32,1,8]{2,1,0:T(1,128)} %broadcast_in_dim.61), calls=%async_computation.12 | async-start | bytes 32768 | tf_op jit(solution)/shard_map/all_to_all | solution.py:16
  335.2 4.5 collective-permute-start.20
  358.8 4.3 collective-permute-start.22
  365.8 6.0 collective-permute-start.24
  367.2 5.9 collective-permute-start.25
  400.9 11.2 %all-to-all-start.16 = ((f32[32,1,8]{2,1,0:T(1,128)}), f32[32,1,8]{2,1,0:T(1,128)S(1)}, u32[]{:S(2)}, u32[]{:S(2)}) async-start(f32[32,1,8]{2,1,0:T(1,128)} %broadcast_in_dim.65), calls=%async_computation.16 | async-start | bytes 32768 | tf_op jit(solution)/shard_map/all_to_all | solution.py:16
  431.3 4.6 collective-permute-start.26
  432.6 4.4 collective-permute-start.27
  471.9 7.4 %collective-permute-start.30 = (f32[8,1,32,128]{3,2,1,0:T(8,128)S(1)}, f32[8,1,32,128]{3,2,1,0:T(8,128)S(1)}, u32[]{:S(2)}, u32[]{:S(2)}) collective-permute-start(f32[8,1,32,128]{3,2,1,0:T(8,128)S(1)} %get-tuple-element.60), channel_id=1, source_target_pairs={{4,0},{8,4},{12,8},{16,12},{20,16},{24,20},{28,24},{32,28},{36,32}... | collective-permute-start | bytes 393224 | tf_op jit(solution)/shard_map/ppermute | solution.py:35
  473.2 7.1 %collective-permute-start.31 = (f32[8,1,32,128]{3,2,1,0:T(8,128)S(1)}, f32[8,1,32,128]{3,2,1,0:T(8,128)S(1)}, u32[]{:S(2)}, u32[]{:S(2)}) collective-permute-start(f32[8,1,32,128]{3,2,1,0:T(8,128)S(1)} %get-tuple-element.61), channel_id=1, source_target_pairs={{0,4},{4,8},{8,12},{12,16},{16,20},{20,24},{24,28},{28,32},{32,36}... | collective-permute-start | bytes 393224 | tf_op jit(solution)/shard_map/ppermute | solution.py:33
  503.8 11.2 %all-to-all-start.20 = ((f32[32,1,8]{2,1,0:T(1,128)}), f32[32,1,8]{2,1,0:T(1,128)S(1)}, u32[]{:S(2)}, u32[]{:S(2)}) async-start(f32[32,1,8]{2,1,0:T(1,128)} %broadcast_in_dim.69), calls=%async_computation.20 | async-start | bytes 32768 | tf_op jit(solution)/shard_map/all_to_all | solution.py:16
  529.0 4.3 collective-permute-start.32
  (100 other events, 1447.1 us)
where the time goes:
time: 641 us; the launch traced here: 631 us
  blocking collectives  345 us (54%)
  starting transfers between devices  118 us (18%)
  other arithmetic  92.8 us (14%)
  waiting for transfers between devices  62.6 us (10%)
  local copies, waits for them, and re-layouts  8.47 us (1%)
    all_to_all x17, blocking collectives, copy_for_each(): lax.all_to_all(jnp.broadcast_to(value[None], (peers, *value.shape)), axis...  276 us
    ppermute x17, starting transfers between devices, extended(): lax.ppermute(tail, axis, [(i, (i + 1) % count) for i in range(ends)])  59.9 us
    psum x4, blocking collectives, over_axes(): value = lax.psum(value, axis)  49.3 us
    all_to_all x7, waiting for transfers between devices, copy_for_each(): lax.all_to_all(jnp.broadcast_to(value[None], (peers, *value.shape)), axis...  45.5 us
    all_to_all x7, starting transfers between devices, copy_for_each(): lax.all_to_all(jnp.broadcast_to(value[None], (peers, *value.shape)), axis...  34.9 us
    ppermute x17, starting transfers between devices, extended(): lax.ppermute(head, axis, [((i + 1) % count, i) for i in range(ends)])  22.9 us
    reduce_sum x6, other arithmetic, inner(): summed = jnp.sum(summed, axis=0)  21.1 us
    all_to_all x1, blocking collectives, body(): lax.all_to_all(hess_block, 'dir', split_axis=2, concat_axis=0, tiled=True)  19.6 us
  transfers between devices with their start and end apart: 41, of which 23 were waited for; matrix products, arithmetic and copies ran while one was open for 1% of the time, Pallas kernels for 0%

commit v1 on v0

v1 whole, which is shorter than its diff:
```python
import functools

import jax
import jax.numpy as jnp
from jax import lax
from jax.experimental import pallas as pl
from jax.experimental.pallas import tpu as pltpu
from jax.sharding import PartitionSpec as P

MESH = pl.DeviceIdType.MESH
F32 = jnp.float32
NCLASS = 8
LANES = 128
SUB = 8
OWN = 8
NL = 16
K = 7
O = K
E = K + NL
LT = NL + 2 * K
HV = 2
ND = SUB // HV
NEAR = 2
NRED = 6


def kernel(
    ns,
    nd,
    cells,
    probes,
    bs_in,
    obs_in,
    perm_in,
    mat_in,
    t_storage,
    t_alpha,
    t_bulk,
    t_shear,
    hess,
    gram,
    praw,
    c_bs,
    c_obs,
    c_perm,
    c_mat,
    c_diag,
    c_stab,
    c_hb,
    c_shear,
    c_tmp,
    pd,
    px,
    py,
    pz,
    pm,
    ed,
    ex,
    ey,
    ez,
    em,
    hb,
    st,
    f,
    w,
    v,
    p1,
    b,
    we,
    r2,
    w2,
    ybuf,
    hraw,
    grecv,
    red_src,
    red_buf,
    ga_src,
    ga_buf,
    gb_src,
    gb_buf,
    sem_init_send,
    sem_part,
    sem_halo,
    sem_loc,
    sem_red_send,
    sem_red,
    sem_ga_send,
    sem_ga,
    sem_gb_send,
    sem_gb,
    sem_g_send,
    sem_g,
    sem_h,
    sem_f_send,
    sem_f,
):
    yh = probes.shape[2] // HV
    ny = probes.shape[2]
    t = lax.axis_index("tile")
    d = lax.axis_index("dir")
    s = t // 2
    c = lax.rem(t, 2)
    partner = s * 2 + (1 - c)
    has_low = s > 0
    has_high = s < ns - 1

    barrier = pltpu.get_barrier_semaphore()

    def greet(tile, dr):
        pl.semaphore_signal(barrier, inc=1, device_id=(tile, dr), device_id_type=MESH)

    for j in range(1, ns):
        greet(lax.rem(s + j, ns) * 2 + c, d)
    greet(partner, d)
    for j in range(1, nd):
        dj = lax.rem(d + j, nd)
        greet(t, dj)
        greet(partner, dj)
    cross = jnp.where(c == 0, s - 1, s + 1)
    has_cross = jnp.where(c == 0, has_low, has_high)

    @pl.when(has_cross)
    def _():
        greet(cross * 2 + (1 - c), d)

    own_at = O + OWN * c
    locals_ = []
    for i, (src, dst) in enumerate(
        (
            (probes.at[pl.ds(ND * c, ND)], praw.at[:, pl.ds(own_at, OWN)]),
            (perm_in, c_perm.at[pl.ds(own_at, OWN)]),
            (mat_in, c_mat.at[pl.ds(own_at, OWN)]),
            (bs_in, c_bs.at[pl.ds(own_at, OWN)]),
            (obs_in, c_obs.at[pl.ds(own_at, OWN)]),
        )
    ):
        cp = pltpu.make_async_copy(src, dst, sem_loc.at[i])
        cp.start()
        locals_.append(cp)

    zero8 = jnp.zeros((SUB, LANES), F32)
    zc = jnp.zeros((ny, LANES), F32)
    zi = jnp.zeros((ny, LANES), jnp.int32)

    def zero_side(lo):
        def layer(i, carry):
            l = lo + i
            for ref in (c_perm, c_bs):
                ref[l] = zc
            c_mat[l] = zi
            for dd in range(ND):
                praw[dd, l] = zc
            for y in range(yh):
                w[l, y] = zero8
                v[l, y] = zero8
                r2[l, y] = zero8
                w2[l, y] = zero8
                for k in range(3):
                    we[k, l, y] = zero8
            return carry

        lax.fori_loop(0, K, layer, 0)

    @pl.when(jnp.logical_not(has_low))
    def _():
        zero_side(0)
        for i in range(NEAR):
            c_obs[O - 1 - i] = zc

    @pl.when(jnp.logical_not(has_high))
    def _():
        zero_side(E)
        for i in range(NEAR):
            c_obs[E + i] = zc

    pl.semaphore_wait(barrier, (ns - 1) + 1 + 2 * (nd - 1) + jnp.where(has_cross, 1, 0))

    def remote(src, dst, ssem, rsem, tile, dr):
        return pltpu.make_async_remote_copy(
            src_ref=src,
            dst_ref=dst,
            send_sem=ssem,
            recv_sem=rsem,
            device_id=(tile, dr),
            device_id_type=MESH,
        )

    part = [
        remote(
            probes.at[pl.ds(ND * (1 - c), ND)],
            praw.at[:, pl.ds(own_at, OWN)],
            sem_init_send.at[0],
            sem_part.at[0],
            partner,
            d,
        )
    ]
    for i, (src, dst) in enumerate(
        ((perm_in, c_perm), (mat_in, c_mat), (bs_in, c_bs), (obs_in, c_obs))
    ):
        part.append(
            remote(
                src,
                dst.at[pl.ds(own_at, OWN)],
                sem_init_send.at[1 + i],
                sem_part.at[1 + i],
                partner,
                d,
            )
        )
    for cp in part:
        cp.start()

    side = 1 - c

    def halo_copies(side, src_near, dst_near, src_far, dst_far, slab):
        out = []
        n = 0
        for far in (False, True):
            at, to, size = (src_far, dst_far, K - NEAR) if far else (src_near, dst_near, NEAR)
            m = 0
            for src, dst in (
                (perm_in, c_perm),
                (mat_in, c_mat),
                (bs_in, c_bs),
                (None, praw),
                (obs_in, c_obs),
            ):
                if far and src is obs_in:
                    continue
                for core in range(2):
                    if src is None:
                        a = probes.at[pl.ds(ND * core, ND), pl.ds(at, size)]
                        z = praw.at[:, pl.ds(to, size)]
                    else:
                        a = src.at[pl.ds(at, size)]
                        z = dst.at[pl.ds(to, size)]
                    out.append(
                        (
                            core,
                            far,
                            remote(
                                a,
                                z,
                                sem_init_send.at[5 + n],
                                sem_halo.at[side, (5 if far else 0) + m],
                                slab * 2 + core,
                                d,
                            ),
                        )
                    )
                    n += 1
                m += 1
        return out

    sends = halo_copies(
        side,
        (OWN - NEAR) * c,
        jnp.where(c == 0, E, O - NEAR),
        jnp.where(c == 0, NEAR, OWN - K),
        jnp.where(c == 0, E + NEAR, 0),
        cross,
    )

    @pl.when(has_cross)
    def _():
        for _, _, cp in sends:
            cp.start()

    low_recv = halo_copies(0, OWN - NEAR, O - NEAR, OWN - K, 0, s)
    high_recv = halo_copies(1, 0, E, NEAR, E + NEAR, s)

    def wait_halo(far):
        @pl.when(has_low)
        def _():
            for core, fr, cp in low_recv:
                if core == 0 and fr == far:
                    cp.wait_recv()

        @pl.when(has_high)
        def _():
            for core, fr, cp in high_recv:
                if core == 0 and fr == far:
                    cp.wait_recv()

    for cp in locals_:
        cp.wait()
    for cp in part:
        cp.wait_recv()
    wait_halo(False)
    wait_halo(True)

    lane = lax.broadcasted_iota(jnp.int32, (SUB, LANES), 1)
    sub = lax.broadcasted_iota(jnp.int32, (SUB, LANES), 0)
    part_of = sub // ND
    lane_c = lax.broadcasted_iota(jnp.int32, (ny, LANES), 1)
    row_c = lax.broadcasted_iota(jnp.int32, (ny, LANES), 0)
    last_z = lane == LANES - 1
    first_z = lane == 0

    def tables(l, carry):
        m = c_mat[l]
        inside = jnp.logical_and(
            jnp.logical_or(has_low, l >= O), jnp.logical_or(has_high, l < E)
        )
        gate = jnp.where(inside, F32(1.0), F32(0.0))

        def look(table):
            val = jnp.full((ny, LANES), table[0], F32)
            for k in range(1, NCLASS):
                val = jnp.where(m == k, table[k], val)
            return val

        storage = look(t_storage)
        biot = look(t_alpha)
        bulk = look(t_bulk)
        shear = look(t_shear)
        stab = biot * biot / bulk
        c_stab[l] = stab
        c_diag[l] = (storage + stab) * gate
        c_hb[l] = 0.5 * biot * gate
        c_shear[l] = shear * gate
        return carry

    lax.fori_loop(0, LT, tables, 0)

    def spread_rows(dst, l, idx, rows=None):
        for y in range(yh if rows is None else rows):
            val = jnp.broadcast_to(c_tmp[idx, pl.ds(y, 1), :], (SUB, LANES))
            for h in range(1, HV):
                more = jnp.broadcast_to(c_tmp[idx, pl.ds(y + h * yh, 1), :], (SUB, LANES))
                val = jnp.where(part_of >= h, more, val)
            dst[l, y] = val

    def faces(src, diag, dd, dx, dy, dz, dm):
        def layer(i, carry):
            l = 1 + i
            mid = src[l]
            xp = 0.5 * (mid + src[l + 1])
            xm = 0.5 * (mid + src[l - 1])
            up = jnp.where(row_c == ny - 1, 0.0, pltpu.roll(mid, ny - 1, 0))
            dn = jnp.where(row_c == 0, 0.0, pltpu.roll(mid, 1, 0))
            yp = 0.5 * (mid + up)
            ym = 0.5 * (mid + dn)
            rt = jnp.where(lane_c == LANES - 1, 0.0, pltpu.roll(mid, LANES - 1, 1))
            lf = jnp.where(lane_c == 0, 0.0, pltpu.roll(mid, 1, 1))
            zp = 0.5 * (mid + rt)
            zm = 0.5 * (mid + lf)
            total = xp + xm + yp + ym + zp + zm
            if diag is not None:
                total = total + diag[l]
            c_tmp[0, 0:ny] = total
            c_tmp[1, 0:ny] = xp
            c_tmp[2, 0:ny] = ym
            c_tmp[2, ny : ny + SUB] = jnp.zeros((SUB, LANES), F32)
            c_tmp[3, 0:ny] = jnp.where(lane_c == LANES - 1, 0.0, zp)
            c_tmp[4, 0:ny] = jnp.where(lane_c == 0, 0.0, zm)
            spread_rows(dd, l, 0)
            spread_rows(dx, l, 1)
            spread_rows(dy, l, 2, yh + 1)
            spread_rows(dz, l, 3)
            spread_rows(dm, l, 4)
            return carry

        lax.fori_loop(0, LT - 2, layer, 0)
        c_tmp[1, 0:ny] = 0.5 * (src[0] + src[1])
        spread_rows(dx, 0, 1)

    faces(c_perm, c_diag, pd, px, py, pz, pm)
    faces(c_shear, None, ed, ex, ey, ez, em)

    def plain(i, carry):
        l = 1 + i
        c_tmp[0, 0:ny] = c_hb[l]
        c_tmp[1, 0:ny] = c_stab[l]
        spread_rows(hb, l, 0)
        spread_rows(st, l, 1)
        return carry

    lax.fori_loop(0, LT - 2, plain, 0)

    def row_of(ref, l, y):
        val = jnp.broadcast_to(ref[l, pl.ds(y, 1), :], (SUB, LANES))
        for h in range(1, HV):
            more = jnp.broadcast_to(ref[l, pl.ds(y + h * yh, 1), :], (SUB, LANES))
            val = jnp.where(part_of >= h, more, val)
        return val

    flat = praw.reshape(ND * LT * ny, LANES)

    def source(l, carry):
        for y in range(yh):
            pieces = [
                flat[pl.ds(l * ny + h * yh + y, ND, stride=LT * ny), :] for h in range(HV)
            ]
            f[l, y] = jnp.concatenate(pieces, axis=0) * row_of(c_bs, l, y)
        return carry

    lax.fori_loop(0, LT, source, 0)

    class Rows:
        def __init__(self, ref, l0, pre=()):
            self.ref, self.l0, self.pre, self.got = ref, l0, pre, {}

        def __call__(self, g, y):
            if (g, y) not in self.got:
                if y == -1:
                    self.got[g, y] = jnp.where(
                        part_of > 0, pltpu.roll(self(g, yh - 1), ND, 0), 0.0
                    )
                elif y == yh:
                    self.got[g, y] = jnp.where(
                        part_of < HV - 1, pltpu.roll(self(g, 0), SUB - ND, 0), 0.0
                    )
                else:
                    self.got[g, y] = self.ref[(*self.pre, self.l0 + g, y)]
            return self.got[g, y]

    def left(x):
        return pltpu.roll(x, 1, 1)

    def right(x):
        return pltpu.roll(x, LANES - 1, 1)

    class Coef:
        def __init__(self, ref, l0):
            self.ref, self.l0, self.got = ref, l0, {}

        def __call__(self, g, y):
            if (g, y) not in self.got:
                self.got[g, y] = self.ref[self.l0 + g, y]
            return self.got[g, y]

    p_ops = (pd, px, py, pz, pm)
    e_ops = (ed, ex, ey, ez, em)

    def group(ops, vals, l0, n, emit):
        cd, cx, cy, cz, cm = (Coef(o, l0) for o in ops)
        for y in range(yh):
            for g in range(n):
                for k, val in enumerate(vals):
                    x = val(g, y)
                    out = cd(g, y) * x
                    out = out - cz(g, y) * right(x)
                    out = out - cm(g, y) * left(x)
                    out = out - cx(g, y) * val(g + 1, y)
                    out = out - cx(g - 1, y) * val(g - 1, y)
                    out = out - cy(g, y + 1) * val(g, y + 1)
                    out = out - cy(g, y) * val(g, y - 1)
                    emit(k, g, y, x, out)

    def rows(ref, l0, k=None):
        return Rows(ref, l0, () if k is None else (k,))

    def own_loop(n, body, init):
        return lax.fori_loop(0, NL // n, lambda i, a: body(O + i * n, n, a), init)

    def halo_loop(k, n, body, far=0):
        trips = (k - far) // n

        @pl.when(has_low)
        def _():
            lax.fori_loop(0, trips, lambda i, a: body(O - k + i * n, n, a), 0)

        @pl.when(has_high)
        def _():
            lax.fori_loop(0, trips, lambda i, a: body(E + far + i * n, n, a), 0)

    zeros = (zero8,)

    def first_pass(ops, src, dst, comps, n):
        def body(l0, n, acc):
            acc = list(acc)

            def emit(k, g, y, x, out):
                if comps is None:
                    dst[l0 + g, y] = out
                else:
                    dst[k, l0 + g, y] = out
                acc[0] = acc[0] + x * x
                acc[1] = acc[1] + x * out
                acc[2] = acc[2] + out * out

            ks = [None] if comps is None else range(comps)
            group(ops, [rows(src, l0, k) for k in ks], l0, n, emit)
            return tuple(acc)

        return own_loop(n, body, zeros * 3)

    def halo_pass(ops, src, dst, comps, k, n, far=0):
        def body(l0, n, acc):
            def emit(kk, g, y, x, out):
                if comps is None:
                    dst[l0 + g, y] = out
                else:
                    dst[kk, l0 + g, y] = out

            ks = [None] if comps is None else range(comps)
            group(ops, [rows(src, l0, kk) for kk in ks], l0, n, emit)
            return acc

        halo_loop(k, n, body, far)

    def second_pass(ops, src, comps, n, dst=None):
        def body(l0, n, acc):
            acc = list(acc)

            def emit(k, g, y, x, out):
                acc[0] = acc[0] + x * out
                if dst is not None:
                    dst[l0 + g, y] = out

            ks = [None] if comps is None else range(comps)
            group(ops, [rows(src, l0, k) for k in ks], l0, n, emit)
            return tuple(acc)

        return own_loop(n, body, zeros)

    GAP = LANES // SUB
    packed_at = lane // GAP == sub

    def red_copy(r, j):
        peer = lax.rem(s + j, ns)
        return remote(
            red_src.at[r],
            red_buf.at[r, s],
            sem_red_send.at[r, j],
            sem_red.at[r, s],
            peer * 2 + c,
            d,
        )

    def red_start(r, moments):
        row = jnp.zeros((SUB, LANES), F32)
        for m, acc in enumerate(moments):
            total = jnp.sum(acc, axis=1, keepdims=True)
            row = row + jnp.where(
                jnp.logical_and(packed_at, lax.rem(lane, GAP) == m), total, 0.0
            )
        packed = jnp.sum(row, axis=0, keepdims=True)
        red_src[r] = packed
        red_buf[r, s] = packed
        for j in range(1, ns):
            red_copy(r, j).start()

    def red_wait(r):
        for j in range(1, ns):
            peer = lax.rem(s + j, ns)
            remote(
                red_src.at[r],
                red_buf.at[r, peer],
                sem_red_send.at[r, j],
                sem_red.at[r, peer],
                peer * 2 + c,
                d,
            ).wait_recv()
        total = red_buf[r, 0]
        for j in range(1, ns):
            total = total + red_buf[r, j]
        full = jnp.where(packed_at, jnp.broadcast_to(total, (SUB, LANES)), 0.0)
        out = []
        for m in range(4):
            val = jnp.sum(
                jnp.where(lax.rem(lane, GAP) == m, full, 0.0), axis=1, keepdims=True
            )
            val = jnp.broadcast_to(val, (SUB, LANES))
            both = val
            for h in range(1, HV):
                both = both + pltpu.roll(val, ND * h, 0)
            out.append(both)
        return out

    def weights(moments):
        m0, m1, m2, m3 = moments
        a0 = m0 / m1
        rr = a0 * a0 * m2 - m0
        beta1 = 1.0 + rr / m0
        dw = beta1 * beta1 * m1 - 2.0 * beta1 * a0 * m2 + a0 * a0 * m3
        a1 = rr / dw
        return a0 + a1 * beta1, -a1 * a0

    def solve(idx, kf, before_halo):
        mo = first_pass(p_ops, f, w, None, 2)
        halo_pass(p_ops, f, w, None, 1, 1)
        (m3,) = second_pass(p_ops, w, None, 2, v)
        red_start(3 * idx, (*mo, m3))
        before_halo()
        halo_pass(p_ops, f, w, None, kf - 1, 1, 1)
        halo_pass(p_ops, w, v, None, kf - 4, 1)
        y0, y1 = weights(red_wait(3 * idx))

        def press(i, a):
            l = O - (kf - 1) + i
            for y in range(yh):
                p1[l, y] = y0 * f[l, y] + y1 * w[l, y]
            return a

        lax.fori_loop(0, NL + 2 * (kf - 1), press, 0)

        def grad(i, a):
            l0 = O - (kf - 2) + 2 * i
            val = rows(p1, l0)
            for y in range(yh):
                for g in range(2):
                    coef = hb[l0 + g, y]
                    x = val(g, y)
                    b[0, l0 + g, y] = coef * (val(g + 1, y) - val(g - 1, y))
                    b[1, l0 + g, y] = coef * (val(g, y + 1) - val(g, y - 1))
                    b[2, l0 + g, y] = coef * (
                        jnp.where(last_z, 0.0, right(x)) - jnp.where(first_z, 0.0, left(x))
                    )
            return a

        lax.fori_loop(0, (NL + 2 * (kf - 2)) // 2, grad, 0)
        mo = first_pass(e_ops, b, we, 3, 1)
        halo_pass(e_ops, b, we, 3, 1, 1)
        (m3,) = second_pass(e_ops, we, 3, 1)
        red_start(3 * idx + 1, (*mo, m3))
        halo_pass(e_ops, b, we, 3, kf - 3, 1, 1)
        z0, z1 = weights(red_wait(3 * idx + 1))

        def resid(l0, n, a):
            got = {}

            def flow(k, g, y):
                if (k, g, y) not in got:
                    if y == -1:
                        got[k, g, y] = jnp.where(
                            part_of > 0, pltpu.roll(flow(k, g, yh - 1), ND, 0), 0.0
                        )
                    elif y == yh:
                        got[k, g, y] = jnp.where(
                            part_of < HV - 1, pltpu.roll(flow(k, g, 0), SUB - ND, 0), 0.0
                        )
                    else:
                        l = l0 + g
                        got[k, g, y] = hb[l, y] * (z0 * b[k, l, y] + z1 * we[k, l, y])
                return got[k, g, y]

            for y in range(yh):
                for g in range(n):
                    l = l0 + g
                    tz = flow(2, g, y)
                    div = flow(0, g - 1, y) - flow(0, g + 1, y)
                    div = div + (flow(1, g, y - 1) - flow(1, g, y + 1))
                    div = div + (
                        jnp.where(first_z, 0.0, left(tz)) - jnp.where(last_z, 0.0, right(tz))
                    )
                    image = y0 * w[l, y] + y1 * v[l, y]
                    r2[l, y] = f[l, y] - div + st[l, y] * p1[l, y] - image
            return a

        own_loop(2, resid, 0)
        halo_loop(kf - 4, 1, resid)

        mo = first_pass(p_ops, r2, w2, None, 2)
        halo_pass(p_ops, r2, w2, None, 1, 1)
        (m3,) = second_pass(p_ops, w2, None, 2)
        red_start(3 * idx + 2, (*mo, m3))
        if kf - 5 > 1:
            halo_pass(p_ops, r2, w2, None, kf - 5, 1, 1)
        return weights(red_wait(3 * idx + 2))

    y0, y1 = solve(0, K, lambda: None)

    def update(i, a):
        l = O - NEAR + i
        for y in range(yh):
            p2 = p1[l, y] + y0 * r2[l, y] + y1 * w2[l, y]
            f[l, y] = p2 * row_of(c_obs, l, y)
        return a

    lax.fori_loop(0, NL + 2 * NEAR, update, 0)

    FAR = K - 1 - NEAR
    to_low = remote(
        f.at[pl.ds(O + NEAR, FAR)],
        f.at[pl.ds(E + NEAR, FAR)],
        sem_f_send.at[0],
        sem_f.at[1],
        jnp.where(has_low, t - 2, t + 2),
        d,
    )
    to_high = remote(
        f.at[pl.ds(E - NEAR - FAR, FAR)],
        f.at[pl.ds(O - NEAR - FAR, FAR)],
        sem_f_send.at[1],
        sem_f.at[0],
        jnp.where(has_high, t + 2, t - 2),
        d,
    )

    @pl.when(has_low)
    def _():
        to_low.start()

    @pl.when(has_high)
    def _():
        to_high.start()

    def new_halo():
        @pl.when(has_low)
        def _():
            to_high.wait_recv()

        @pl.when(has_high)
        def _():
            to_low.wait_recv()

    y0, y1 = solve(1, K - 1, new_halo)

    def finish(i, a):
        l = O + i
        for y in range(yh):
            p2 = p1[l, y] + y0 * r2[l, y] + y1 * w2[l, y]
            ybuf[i, y] = p2 * row_of(c_bs, l, y)
        return a

    lax.fori_loop(0, NL, finish, 0)

    me = d * 2 + c
    nq = 2 * nd
    per = NL // nq

    def gram_copy(q, slot):
        dq = q // 2
        cq = lax.rem(q, 2)
        return remote(
            ybuf.at[pl.ds(per * q, per)],
            grecv.at[slot],
            sem_g_send.at[q],
            sem_g.at[slot],
            s * 2 + cq,
            dq,
        )

    for j in range(1, nq):
        gram_copy(lax.rem(me + j, nq), me).start()

    hflat = hraw.reshape(ND * OWN * ny, LANES)
    oflat = hess.reshape(2 * ND * OWN * ny, LANES)

    def unpack(dst, base, at):
        def layer(i, a):
            for y in range(yh):
                val = ybuf[at + i, y]
                for h in range(HV):
                    dst[pl.ds(base + i * ny + h * yh + y, ND, stride=OWN * ny), :] = val[
                        h * ND : (h + 1) * ND
                    ]
            return a

        lax.fori_loop(0, OWN, layer, 0)

    unpack(hflat, 0, OWN * (1 - c))
    swap = remote(
        hraw,
        hess.at[pl.ds(ND * c, ND)],
        sem_h.at[0],
        sem_h.at[1],
        partner,
        d,
    )
    swap.start()
    unpack(oflat, ND * c * OWN * ny, OWN * c)

    for i in range(per):
        for y in range(yh):
            grecv[me, i, y] = ybuf[per * me + i, y]
    for j in range(1, nq):
        q = lax.rem(me + j, nq)
        gram_copy(q, q).wait_recv()

    width = nq * SUB

    def gram_part(i, acc):
        for l in range(per):
            z = grecv[:, l, i].reshape(width, LANES)
            acc = acc + lax.dot_general(
                z,
                z,
                (((1,), (1,)), ((), ())),
                precision=lax.Precision.HIGHEST,
                preferred_element_type=F32,
            )
        return acc

    g64 = lax.fori_loop(0, yh, gram_part, jnp.zeros((width, width), F32))
    ndir = nq * ND
    fold = jnp.zeros((ndir, LANES), F32)
    for h in range(HV):
        ri = lax.broadcasted_iota(jnp.int32, (ndir, width), 0)
        ci = lax.broadcasted_iota(jnp.int32, (ndir, width), 1)
        left_sel = jnp.where(ci == (ri // ND) * SUB + h * ND + lax.rem(ri, ND), 1.0, 0.0)
        rj = lax.broadcasted_iota(jnp.int32, (width, LANES), 0)
        cj = lax.broadcasted_iota(jnp.int32, (width, LANES), 1)
        right_sel = jnp.where(
            jnp.logical_and(rj == (cj // ND) * SUB + h * ND + lax.rem(cj, ND), cj < ndir),
            1.0,
            0.0,
        )
        mid = jnp.dot(
            left_sel, g64, precision=lax.Precision.HIGHEST, preferred_element_type=F32
        )
        fold = fold + jnp.dot(
            mid, right_sel, precision=lax.Precision.HIGHEST, preferred_element_type=F32
        )
    packed = fold[0:SUB]
    for k in range(1, ndir // SUB):
        packed = packed + pltpu.roll(fold[k * SUB : (k + 1) * SUB], ndir * k, 1)

    ga_src[...] = packed
    ga_buf[s] = packed

    def ga_copy(j, slot):
        peer = lax.rem(s + j, ns)
        return remote(
            ga_src, ga_buf.at[slot], sem_ga_send.at[j], sem_ga.at[slot], peer * 2 + c, d
        )

    for j in range(1, ns):
        ga_copy(j, s).start()
    for j in range(1, ns):
        ga_copy(j, lax.rem(s + j, ns)).wait_recv()
    total = ga_buf[0]
    for j in range(1, ns):
        total = total + ga_buf[j]
    gb_src[...] = total
    gb_buf[me] = total

    def gb_copy(j, slot):
        q = lax.rem(me + j, nq)
        return remote(
            gb_src,
            gb_buf.at[slot],
            sem_gb_send.at[j],
            sem_gb.at[slot],
            s * 2 + lax.rem(q, 2),
            q // 2,
        )

    for j in range(1, nq):
        gb_copy(j, me).start()
    for j in range(1, nq):
        gb_copy(j, lax.rem(me + j, nq)).wait_recv()
    total = gb_buf[0]
    for j in range(1, nq):
        total = total + gb_buf[j]
    total = total * (1.0 / cells)
    for k in range(ndir // SUB):
        row = total if k == 0 else pltpu.roll(total, LANES - ndir * k, 1)
        gram[k * SUB : (k + 1) * SUB] = row

    swap.wait_recv()
    swap.wait_send()
    for cp in part:
        cp.wait_send()

    @pl.when(has_cross)
    def _():
        for _, _, cp in sends:
            cp.wait_send()

    for r in range(NRED):
        for j in range(1, ns):
            red_copy(r, j).wait_send()

    @pl.when(has_low)
    def _():
        to_low.wait_send()

    @pl.when(has_high)
    def _():
        to_high.wait_send()

    for j in range(1, nq):
        gram_copy(lax.rem(me + j, nq), me).wait_send()
    for j in range(1, ns):
        ga_copy(j, s).wait_send()
    for j in range(1, nq):
        gb_copy(j, me).wait_send()


def solution(mesh):
    ns = mesh.shape["tile"] // 2
    nd = mesh.shape["dir"]
    nq = 2 * nd

    def body(probes, bs, obs, perm, mat, storage, alpha, bulk, shear):
        ny, nz = probes.shape[2:]
        yh = ny // HV
        cells = OWN * 2 * ns * ny * nz
        vm = pl.BlockSpec(memory_space=pltpu.VMEM)
        sm = pl.BlockSpec(memory_space=pltpu.SMEM)

        def compact(n=LT, kind=F32):
            return pltpu.VMEM((n, ny, nz), kind)

        def wide(rows=yh, pre=()):
            return pltpu.VMEM((*pre, LT, rows, SUB, nz), F32)

        dma = pltpu.SemaphoreType.DMA
        scratch = [
            pltpu.VMEM((ND, LT, ny, nz), F32),
            compact(),
            compact(),
            compact(),
            compact(kind=jnp.int32),
            compact(),
            compact(),
            compact(),
            compact(),
            pltpu.VMEM((5, ny + SUB, nz), F32),
            wide(),
            wide(),
            wide(yh + 1),
            wide(),
            wide(),
            wide(),
            wide(),
            wide(yh + 1),
            wide(),
            wide(),
            wide(),
            wide(),
            wide(),
            wide(),
            wide(),
            wide(),
            wide(pre=(3,)),
            wide(pre=(3,)),
            wide(),
            wide(),
            pltpu.VMEM((NL, yh, SUB, nz), F32),
            pltpu.VMEM((ND, OWN, ny, nz), F32),
            pltpu.VMEM((nq, NL // nq, yh, SUB, nz), F32),
            pltpu.VMEM((NRED, 1, nz), F32),
            pltpu.VMEM((NRED, ns, 1, nz), F32),
            pltpu.VMEM((SUB, nz), F32),
            pltpu.VMEM((ns, SUB, nz), F32),
            pltpu.VMEM((SUB, nz), F32),
            pltpu.VMEM((nq, SUB, nz), F32),
            dma((5 + 18,)),
            dma((5,)),
            dma((2, 9)),
            dma((5,)),
            dma((NRED, ns)),
            dma((NRED, ns)),
            dma((ns,)),
            dma((ns,)),
            dma((nq,)),
            dma((nq,)),
            dma((nq,)),
            dma((nq,)),
            dma((2,)),
            dma((2,)),
            dma((2,)),
        ]
        hess, gram = pl.pallas_call(
            functools.partial(kernel, ns, nd, cells),
            out_shape=(
                jax.ShapeDtypeStruct(probes.shape, F32),
                jax.ShapeDtypeStruct((nq * ND, nz), F32),
            ),
            in_specs=[vm] * 5 + [sm] * 4,
            out_specs=(vm, vm),
            scratch_shapes=scratch,
            compiler_params=pltpu.CompilerParams(
                collective_id=0, has_side_effects=True, vmem_limit_bytes=67043328
            ),
        )(probes, bs, obs, perm, mat, storage, alpha, bulk, shear)
        r_factor = jnp.linalg.cholesky(gram[:, : nq * ND]).T
        return hess, r_factor

    return jax.shard_map(
        body,
        mesh=mesh,
        in_specs=(
            P("dir", "tile", None, None),
            P("tile", None, None),
            P("tile", None, None),
            P("tile", None, None),
            P("tile", None, None),
            P(),
            P(),
            P(),
            P(),
        ),
        out_specs=(P("dir", "tile", None, None), P()),
        check_vma=False,
    )
```

time: 641 us -> 139 us (0.22); the launches traced: 631 us -> 137 us
  blocking collectives: 345 us -> 0 us
  Pallas kernels: 0 us -> 129 us
  starting transfers between devices: 118 us -> 0 us
  other arithmetic: 92.8 us -> 4.25 us
  waiting for transfers between devices: 62.6 us -> 0 us
    all_to_all x18 -> x0, blocking collectives: 296 us -> none  [the longest x17 276 us: copy_for_each(): lax.all_to_all(jnp.broadcast_to(value[None], (peers, *value.shape)), axis...]
    pallas_call x0 -> x1, Pallas kernels: none -> 129 us  [body(): pl.pallas_call(functools.partial(kernel, ns, nd, cells), out_shape=(jax.S...]
    ppermute x34 -> x0, starting transfers between devices: 82.8 us -> none  [the longest x17 59.9 us: extended(): lax.ppermute(tail, axis, [(i, (i + 1) % count) for i in range(ends)])]
    psum x4 -> x0, blocking collectives: 49.3 us -> none  [over_axes(): value = lax.psum(value, axis)]
    reduce_sum x43 -> x0, other arithmetic: 47.5 us -> none  [the longest x6 21.1 us: inner(): summed = jnp.sum(summed, axis=0)]
    all_to_all x7 -> x0, waiting for transfers between devices: 45.5 us -> none  [copy_for_each(): lax.all_to_all(jnp.broadcast_to(value[None], (peers, *value.shape)), axis...]
    all_to_all x7 -> x0, starting transfers between devices: 34.9 us -> none  [copy_for_each(): lax.all_to_all(jnp.broadcast_to(value[None], (peers, *value.shape)), axis...]
    add x10 -> x0, other arithmetic: 17.8 us -> none  [the longest x6 11.7 us: conj_grad(): direction = residual + spread(norm_next / norm_now) * direction]
  transfers between devices with their start and end apart: 41 -> 0, of which waited for: 23 -> 0; matrix products, arithmetic and copies ran while one was open for 1% -> 0% of each run, Pallas kernels for 0% -> 0%
where the time goes in v1:
time: 139 us; the launch traced here: 137 us
  Pallas kernels  129 us (93%)
  other arithmetic  4.25 us (3%)
  local copies, waits for them, and re-layouts  3.83 us (3%)
    pallas_call x1, Pallas kernels, body(): pl.pallas_call(functools.partial(kernel, ns, nd, cells), out_shape=(jax.S...  129 us
    another operation x3, other arithmetic, body(): r_factor = jnp.linalg.cholesky(gram[:, :nq * ND]).T  3.6 us
    unnamed x2, local copies, waits for them, and re-layouts  2.94 us

profile of v1, /device:TPU:0, one launch (start us, length us, event | category | flops | bytes accessed | tf_op | source)
XLA Modules:
  0.0 137.5 jit_solution(5313008355427934384)
XLA Ops:
  0.6 128.7 %shard_map.104 = (f32[8,8,32,128]{3,2,1,0:T(8,128)}, f32[32,128]{1,0:T(8,128)}) custom-call(f32[8,8,32,128]{3,2,1,0:T(8,128)} %probes.1, f32[8,32,128]{2,1,0:T(8,128)} %bs_in.1, f32[8,32,128]{2,1,0:T(8,128)} %obs_in.1, f32[8,32,128]{2,1,0:T(8,128)} %perm_in.1, s32[8,32,128]{2,1,0:T(8,128)} %mat_in.1, f32[8]{0:T(128)} %t_storage.1, f32[8]{0:T(128)} %t_alpha.1, ...), custom_call_target="tpu_custom_call" | custom-call | tf_op jit(solution)/shard_map/pallas_call | solution.py:959
  129.4 0.8 copy.11
  130.2 0.1 copy.12
  130.3 2.9 %cholesky.18 = f32[32,32]{1,0:T(8,128)S(1)} custom-call(f32[32,32]{1,0:T(8,128)S(1)} %fusion), custom_call_target="Cholesky" | custom-call | tf_op jit(solution)/shard_map/jit(cholesky)/cholesky | solution.py:972
  133.2 0.6 compare_reduce_fusion
  133.9 0.6 select_bitcast_fusion
  134.5 0.7 copy.13
  135.2 2.3 %copy.15 = f32[8,8,32,128]{3,2,1,0:T(8,128)} copy(f32[8,8,32,128]{3,2,1,0:T(8,128)} %get-tuple-element.10) | data formatting | bytes 2097152
  (3 shorter events, 0.0 us)

commit v2 on v1

v2 whole, which is shorter than its diff:
```python
import functools

import jax
import jax.numpy as jnp
from jax import lax
from jax.experimental import pallas as pl
from jax.experimental.pallas import tpu as pltpu
from jax.sharding import PartitionSpec as P

MESH = pl.DeviceIdType.MESH
F32 = jnp.float32
NCLASS = 8
LANES = 128
SUB = 8
OWN = 8
NL = 16
K = 6
O = K
E = K + NL
LT = NL + 2 * K
NB = 2
HV = 4
ND = SUB // HV
NDEV = NB * ND
NEAR = 2
NRED = 6 * NB


def kernel(
    ns,
    nd,
    cells,
    probes,
    bs_in,
    obs_in,
    perm_in,
    mat_in,
    t_storage,
    t_alpha,
    t_bulk,
    t_shear,
    hess,
    gram,
    fraw,
    praw,
    c_bs,
    c_obs,
    c_perm,
    c_mat,
    c_diag,
    c_stab,
    c_hb,
    c_shear,
    c_tmp,
    pd,
    px,
    py,
    pz,
    pm,
    ed,
    ex,
    ey,
    ez,
    em,
    hb,
    st,
    f,
    w,
    v,
    p1,
    b,
    we,
    r2,
    w2,
    ybuf,
    hraw,
    grecv,
    wts,
    red_src,
    red_buf,
    ga_src,
    ga_buf,
    gb_src,
    gb_buf,
    sem_init_send,
    sem_part,
    sem_halo,
    sem_red_send,
    sem_red,
    sem_ga_send,
    sem_ga,
    sem_gb_send,
    sem_gb,
    sem_g_send,
    sem_g,
    sem_h,
    sem_f_send,
    sem_f,
    sem_r_send,
    sem_r,
):
    scope = []

    def phase(name=None):
        if scope:
            scope.pop().__exit__(None, None, None)
        if name is not None:
            scope.append(jax.named_scope(name))
            scope[0].__enter__()

    phase("a_start")
    ny = probes.shape[2]
    yh = ny // HV
    t = lax.axis_index("tile")
    d = lax.axis_index("dir")
    s = t // 2
    c = lax.rem(t, 2)
    partner = s * 2 + (1 - c)
    has_low = s > 0
    has_high = s < ns - 1

    barrier = pltpu.get_barrier_semaphore()

    def greet(tile, dr):
        pl.semaphore_signal(barrier, inc=1, device_id=(tile, dr), device_id_type=MESH)

    cross = jnp.where(c == 0, s - 1, s + 1)
    has_cross = jnp.where(c == 0, has_low, has_high)
    for j in range(1, ns):
        greet(lax.rem(s + j, ns) * 2 + c, d)
    greet(partner, d)
    for j in range(1, nd):
        dj = lax.rem(d + j, nd)
        greet(t, dj)
        greet(partner, dj)

    @pl.when(has_cross)
    def _():
        greet(cross * 2 + (1 - c), d)

    own_at = O + OWN * c
    zero8 = jnp.zeros((SUB, LANES), F32)
    zc = jnp.zeros((ny, LANES), F32)
    zi = jnp.zeros((ny, LANES), jnp.int32)

    def products(l, a):
        sens = bs_in[l]
        for dd in range(2 * NDEV):
            fraw[dd, l] = probes[dd, l] * sens
        c_bs[own_at + l] = sens
        c_obs[own_at + l] = obs_in[l]
        c_perm[own_at + l] = perm_in[l]
        c_mat[own_at + l] = mat_in[l]
        return a

    lax.fori_loop(0, OWN, products, 0)

    def zero_side(lo):
        def layer(i, carry):
            l = lo + i
            c_perm[l] = zc
            c_obs[l] = zc
            c_mat[l] = zi
            for dd in range(NDEV):
                praw[dd, l] = zc
            for q in range(NB):
                for y in range(yh):
                    w[q, l, y] = zero8
                    v[q, l, y] = zero8
                    r2[q, l, y] = zero8
                    w2[q, l, y] = zero8
                    for k in range(3):
                        we[q, k, l, y] = zero8
            return carry

        lax.fori_loop(0, K, layer, 0)

    @pl.when(jnp.logical_not(has_low))
    def _():
        zero_side(0)

    @pl.when(jnp.logical_not(has_high))
    def _():
        zero_side(E)

    lane = lax.broadcasted_iota(jnp.int32, (SUB, LANES), 1)
    sub = lax.broadcasted_iota(jnp.int32, (SUB, LANES), 0)
    part_of = sub // ND
    lane_c = lax.broadcasted_iota(jnp.int32, (ny, LANES), 1)
    row_c = lax.broadcasted_iota(jnp.int32, (ny, LANES), 0)
    last_z = lane == LANES - 1
    first_z = lane == 0

    def tables(lo, n):
        def layer(i, carry):
            l = lo + i
            m = c_mat[l]
            inside = jnp.logical_and(
                jnp.logical_or(has_low, l >= O), jnp.logical_or(has_high, l < E)
            )
            gate = jnp.where(inside, F32(1.0), F32(0.0))

            def look(table):
                val = jnp.full((ny, LANES), table[0], F32)
                for k in range(1, NCLASS):
                    val = jnp.where(m == k, table[k], val)
                return val

            biot = look(t_alpha)
            stab = biot * biot / look(t_bulk)
            c_stab[l] = stab
            c_diag[l] = (look(t_storage) + stab) * gate
            c_hb[l] = 0.5 * biot * gate
            c_shear[l] = look(t_shear) * gate
            return carry

        lax.fori_loop(0, n, layer, 0)

    phase("a_tables")
    tables(own_at, OWN)

    phase("b_barrier")
    pl.semaphore_wait(barrier, (ns - 1) + 1 + 2 * (nd - 1) + jnp.where(has_cross, 1, 0))

    def remote(src, dst, ssem, rsem, tile, dr):
        return pltpu.make_async_remote_copy(
            src_ref=src,
            dst_ref=dst,
            send_sem=ssem,
            recv_sem=rsem,
            device_id=(tile, dr),
            device_id_type=MESH,
        )

    def part_copies():
        pairs = ((perm_in, c_perm), (mat_in, c_mat), (None, praw), (bs_in, c_bs), (obs_in, c_obs))
        out = []
        for i, (src, dst) in enumerate(pairs):
            if src is None:
                src = fraw.at[pl.ds(NDEV * (1 - c), NDEV)]
                dst = dst.at[:, pl.ds(own_at, OWN)]
            else:
                dst = dst.at[pl.ds(own_at, OWN)]
            out.append(remote(src, dst, sem_init_send.at[i], sem_part.at[i], partner, d))
        return out

    def halo_copies(side, slab, near, far, cores, only=None):
        jobs = []
        for n, (src, dst) in enumerate(((perm_in, c_perm), (mat_in, c_mat), (None, praw))):
            jobs.append((n, src, dst, *near, NEAR))
        for n, (src, dst) in enumerate(((perm_in, c_perm), (mat_in, c_mat), (None, praw))):
            jobs.append((3 + n, src, dst, *far, K - NEAR))
        jobs.append((6, obs_in, c_obs, *near, NEAR))
        out = []
        for n, src, dst, at, to, size in jobs:
            if only is not None and n not in only:
                continue
            for core in cores:
                if src is None:
                    a = fraw.at[pl.ds(NDEV * core, NDEV), pl.ds(at, size)]
                    z = praw.at[:, pl.ds(to, size)]
                else:
                    a = src.at[pl.ds(at, size)]
                    z = dst.at[pl.ds(to, size)]
                out.append(
                    remote(
                        a,
                        z,
                        sem_init_send.at[5 + 2 * n + core],
                        sem_halo.at[side, n],
                        slab * 2 + core,
                        d,
                    )
                )
        return out

    def cross_copies():
        return halo_copies(
            1 - c,
            cross,
            ((OWN - NEAR) * c, jnp.where(c == 0, E, O - NEAR)),
            (jnp.where(c == 0, NEAR, OWN - K), jnp.where(c == 0, E + NEAR, 0)),
            (0, 1),
        )

    phase("c_sends")

    @pl.when(has_cross)
    def _():
        for cp in cross_copies():
            cp.start()

    for cp in part_copies():
        cp.start()

    def wait_halo(only):
        @pl.when(has_low)
        def _():
            for cp in halo_copies(0, s, (OWN - NEAR, O - NEAR), (OWN - K, 0), (0,), only):
                cp.wait_recv()

        @pl.when(has_high)
        def _():
            for cp in halo_copies(1, s, (0, E), (NEAR, E + NEAR), (0,), only):
                cp.wait_recv()

    def wide_row(read, y):
        val = jnp.broadcast_to(read(y), (SUB, LANES))
        for h in range(1, HV):
            more = jnp.broadcast_to(read(y + h * yh), (SUB, LANES))
            val = jnp.where(part_of >= h, more, val)
        return val

    def row_of(ref, l, y):
        return wide_row(lambda y: ref[l, pl.ds(y, 1), :], y)

    def spread_rows(dst, l, idx, rows=None):
        for y in range(yh if rows is None else rows):
            dst[l, y] = row_of(c_tmp, idx, y)

    def faces_layer(l, src, diag, dd, dx, dy, dz, dm, at):
        mid = src[l]
        xp = 0.5 * (mid + src[l + 1])
        xm = 0.5 * (mid + src[l - 1])
        up = jnp.where(row_c == ny - 1, 0.0, pltpu.roll(mid, ny - 1, 0))
        dn = jnp.where(row_c == 0, 0.0, pltpu.roll(mid, 1, 0))
        yp = 0.5 * (mid + up)
        ym = 0.5 * (mid + dn)
        rt = jnp.where(lane_c == LANES - 1, 0.0, pltpu.roll(mid, LANES - 1, 1))
        lf = jnp.where(lane_c == 0, 0.0, pltpu.roll(mid, 1, 1))
        zp = 0.5 * (mid + rt)
        zm = 0.5 * (mid + lf)
        total = xp + xm + yp + ym + zp + zm
        if diag is not None:
            total = total + diag[l]
        c_tmp[at, 0:ny] = total
        c_tmp[at + 1, 0:ny] = xp
        c_tmp[at + 2, 0:ny] = ym
        c_tmp[at + 2, ny : ny + SUB] = jnp.broadcast_to(
            0.5 * mid[ny - 1 : ny], (SUB, LANES)
        )
        c_tmp[at + 3, 0:ny] = jnp.where(lane_c == LANES - 1, 0.0, zp)
        c_tmp[at + 4, 0:ny] = jnp.where(lane_c == 0, 0.0, zm)
        return lambda: (
            spread_rows(dd, l, at),
            spread_rows(dx, l, at + 1),
            spread_rows(dy, l, at + 2, yh + 1),
            spread_rows(dz, l, at + 3),
            spread_rows(dm, l, at + 4),
        )

    def faces(lo, n):
        def layer(i, carry):
            l = lo + i
            done = (
                faces_layer(l, c_perm, c_diag, pd, px, py, pz, pm, 0),
                faces_layer(l, c_shear, None, ed, ex, ey, ez, em, 5),
            )
            for y in range(yh):
                hb[l, y] = row_of(c_hb, l, y)
                st[l, y] = row_of(c_stab, l, y)
            for make in done:
                make()
            return carry

        lax.fori_loop(0, n, layer, 0)

    def x_faces(l):
        c_tmp[1, 0:ny] = 0.5 * (c_perm[l] + c_perm[l + 1])
        c_tmp[6, 0:ny] = 0.5 * (c_shear[l] + c_shear[l + 1])
        spread_rows(px, l, 1)
        spread_rows(ex, l, 6)

    def source(lo, n, raw=praw, first=0, shift=0, layers=LT):
        flat = raw.reshape(raw.shape[0] * layers * ny, LANES)

        def layer(i, carry):
            l = lo + i
            for q in range(NB):
                for y in range(yh):
                    base = ((first + q * ND) * layers + (l - shift)) * ny + y
                    f[q, l, y] = jnp.concatenate(
                        [
                            flat[pl.ds(base + h * yh, ND, stride=layers * ny), :]
                            for h in range(HV)
                        ],
                        axis=0,
                    )
            return carry

        lax.fori_loop(0, n, layer, 0)

    phase("d_own")
    faces(own_at + 1, OWN - 2)
    source(own_at, OWN, fraw, NDEV * c, own_at, OWN)
    phase("d_wait_part")
    for cp in part_copies():
        cp.wait_recv()
    phase("d_other")
    other_at = O + OWN * (1 - c)
    tables(other_at, OWN)
    faces(jnp.where(c == 0, O + OWN - 1, O + 1), OWN)
    source(other_at, OWN)
    phase("d_wait_near")
    wait_halo((0, 1, 2))
    phase("d_near")
    tables(O - NEAR, NEAR)
    tables(E, NEAR)
    faces(O - 1, 2)
    faces(E - 1, 2)
    x_faces(O - 2)
    source(O - NEAR, NEAR)
    source(E, NEAR)

    def far_layers():
        wait_halo((3, 4, 5))
        tables(0, K - NEAR)
        tables(E + NEAR, K - NEAR)
        faces(1, K - NEAR)
        faces(E + 1, K - NEAR)
        x_faces(0)
        source(0, K - NEAR)
        source(E + NEAR, K - NEAR)

    class Rows:
        def __init__(self, ref, l0, pre=()):
            self.ref, self.l0, self.pre, self.got = ref, l0, pre, {}

        def load(self, g, y):
            return self.ref[(*self.pre, self.l0 + g, y)]

        def __call__(self, g, y):
            if (g, y) not in self.got:
                if y == -1:
                    self.got[g, y] = jnp.where(
                        part_of > 0, pltpu.roll(self(g, yh - 1), ND, 0), 0.0
                    )
                elif y == yh:
                    self.got[g, y] = jnp.where(
                        part_of < HV - 1, pltpu.roll(self(g, 0), SUB - ND, 0), 0.0
                    )
                else:
                    self.got[g, y] = self.load(g, y)
            return self.got[g, y]

    class Made(Rows):
        def __init__(self, make):
            self.make, self.got = make, {}

        def load(self, g, y):
            return self.make(g, y)

    def left(x):
        return pltpu.roll(x, 1, 1)

    def right(x):
        return pltpu.roll(x, LANES - 1, 1)

    p_ops = (pd, px, py, pz, pm)
    e_ops = (ed, ex, ey, ez, em)

    def group(ops, vals, l0, n, emit):
        cd, cx, cy, cz, cm = (Rows(o, l0).load for o in ops)
        cx, cy = Rows(ops[1], l0), Made(cy)
        for y in range(yh):
            for g in range(n):
                co = [
                    op(g, y) for op in (cd, cz, cm)
                ]
                c_up = ops[2][l0 + g, y + 1]
                c_dn = ops[2][l0 + g, y]
                for k, val in enumerate(vals):
                    x = val(g, y)
                    out = co[0] * x
                    out = out - co[1] * right(x)
                    out = out - co[2] * left(x)
                    out = out - cx(g, y) * val(g + 1, y)
                    out = out - cx(g - 1, y) * val(g - 1, y)
                    out = out - c_up * val(g, y + 1)
                    out = out - c_dn * val(g, y - 1)
                    emit(k, g, y, x, out)

    def own_loop(n, body, init):
        return lax.fori_loop(0, NL // n, lambda i, a: body(O + i * n, n, a), init)

    def halo_loop(k, n, body, far=0):
        trips = (k - far) // n

        @pl.when(has_low)
        def _():
            lax.fori_loop(0, trips, lambda i, a: body(O - k + i * n, n, a), 0)

        @pl.when(has_high)
        def _():
            lax.fori_loop(0, trips, lambda i, a: body(E + far + i * n, n, a), 0)

    def pres(q, comps):
        return [(q,)] if comps is None else [(q, k) for k in range(comps)]

    def first_pass(q, ops, src, dst, comps, n):
        pre = pres(q, comps)

        def body(l0, n, acc):
            acc = list(acc)

            def emit(k, g, y, x, out):
                dst[(*pre[k], l0 + g, y)] = out
                acc[0] = acc[0] + x * x
                acc[1] = acc[1] + x * out
                acc[2] = acc[2] + out * out

            group(ops, [Rows(src, l0, k) for k in pre], l0, n, emit)
            return tuple(acc)

        return own_loop(n, body, (zero8,) * 3)

    def halo_pass(q, ops, src, dst, comps, k, n, far=0):
        pre = pres(q, comps)

        def body(l0, n, acc):
            def emit(kk, g, y, x, out):
                dst[(*pre[kk], l0 + g, y)] = out

            group(ops, [Rows(src, l0, kk) for kk in pre], l0, n, emit)
            return acc

        halo_loop(k, n, body, far)

    def second_pass(q, ops, src, comps, n, dst=None):
        pre = pres(q, comps)

        def body(l0, n, acc):
            acc = list(acc)

            def emit(k, g, y, x, out):
                acc[0] = acc[0] + x * out
                if dst is not None:
                    dst[q, l0 + g, y] = out

            group(ops, [Rows(src, l0, k) for k in pre], l0, n, emit)
            return tuple(acc)

        return own_loop(n, body, (zero8,))

    GAP = LANES // SUB
    packed_at = lane // GAP == sub

    def red_copy(r, j, slot):
        peer = lax.rem(s + j, ns)
        return remote(
            red_src.at[r],
            red_buf.at[r, slot],
            sem_red_send.at[r, j],
            sem_red.at[r, slot],
            peer * 2 + c,
            d,
        )

    def red_start(r, moments):
        row = jnp.zeros((SUB, LANES), F32)
        for m, acc in enumerate(moments):
            total = jnp.sum(acc, axis=1, keepdims=True)
            row = row + jnp.where(
                jnp.logical_and(packed_at, lax.rem(lane, GAP) == m), total, 0.0
            )
        packed = jnp.sum(row, axis=0, keepdims=True)
        red_src[r] = packed
        red_buf[r, s] = packed
        for j in range(1, ns):
            red_copy(r, j, s).start()

    def red_wait(r):
        for j in range(1, ns):
            red_copy(r, j, lax.rem(s + j, ns)).wait_recv()
        total = red_buf[r, 0]
        for j in range(1, ns):
            total = total + red_buf[r, j]
        full = jnp.where(packed_at, jnp.broadcast_to(total, (SUB, LANES)), 0.0)
        out = []
        for m in range(4):
            val = jnp.sum(
                jnp.where(lax.rem(lane, GAP) == m, full, 0.0), axis=1, keepdims=True
            )
            val = jnp.broadcast_to(val, (SUB, LANES))
            both = val
            for h in range(1, HV):
                both = both + pltpu.roll(val, ND * h, 0)
            out.append(both)
        return out

    def weights(moments):
        m0, m1, m2, m3 = moments
        a0 = m0 / m1
        rr = a0 * a0 * m2 - m0
        beta1 = 1.0 + rr / m0
        dw = beta1 * beta1 * m1 - 2.0 * beta1 * a0 * m2 + a0 * a0 * m3
        a1 = rr / dw
        return a0 + a1 * beta1, -a1 * a0

    def strip(q, buf, at, to, size, ssem, rsem):
        low = remote(
            buf.at[q, pl.ds(O + at, size)],
            buf.at[q, pl.ds(E + to, size)],
            ssem.at[q, 0],
            rsem.at[q, 1],
            jnp.where(has_low, t - 2, t + 2),
            d,
        )
        high = remote(
            buf.at[q, pl.ds(E - at - size, size)],
            buf.at[q, pl.ds(O - to - size, size)],
            ssem.at[q, 1],
            rsem.at[q, 0],
            jnp.where(has_high, t + 2, t - 2),
            d,
        )
        return low, high

    def strip_do(args, start=False, recv=False, sent=False):
        low, high = strip(*args)

        @pl.when(has_low)
        def _():
            if start:
                low.start()
            if recv:
                high.wait_recv()
            if sent:
                low.wait_send()

        @pl.when(has_high)
        def _():
            if start:
                high.start()
            if recv:
                low.wait_recv()
            if sent:
                high.wait_send()

    def f_strip(q):
        return q, f, NEAR, NEAR, K - NEAR, sem_f_send, sem_f

    def r_strip(q):
        return q, r2, 2, 2, 1, sem_r_send, sem_r

    me = d * 2 + c
    nq = 2 * nd
    per = NL // nq

    def gram_copy(bt, l, q, slot):
        return remote(
            ybuf.at[bt, per * q + l],
            grecv.at[slot, bt, l],
            sem_g_send.at[bt, l, q],
            sem_g.at[bt, l, slot],
            s * 2 + lax.rem(q, 2),
            q // 2,
        )

    def each(stage, *args):
        def go(q, a):
            stage(q, *args)
            return a

        lax.fori_loop(0, NB, go, 0)

    def save(q, at, pair):
        for i in range(2):
            wts[q, at + i] = pair[i]

    def begin(q, base):
        mo = first_pass(q, p_ops, f, w, None, PN)
        halo_pass(q, p_ops, f, w, None, 1, 1)
        (m3,) = second_pass(q, p_ops, w, None, PN, v)
        red_start(base + q, (*mo, m3))

    def begin_far(q, idx):
        @pl.when(idx > 0)
        def _():
            strip_do(f_strip(q), recv=True)

        halo_pass(q, p_ops, f, w, None, K - 1, K - 2, 1)
        halo_pass(q, p_ops, w, v, None, 2, 2)

    def displace(q, base):
        y0, y1 = weights(red_wait(base + q))
        save(q, 0, (y0, y1))

        def press(i, a):
            for g in range(2):
                l = 1 + 2 * i + g
                for y in range(yh):
                    p1[q, l, y] = y0 * f[q, l, y] + y1 * w[q, l, y]
            return a

        lax.fori_loop(0, (LT - 2) // 2, press, 0)

        def grad(i, a):
            l0 = 2 + 4 * i
            val = Rows(p1, l0, (q,))
            for y in range(yh):
                for g in range(4):
                    coef = hb[l0 + g, y]
                    x = val(g, y)
                    b[q, 0, l0 + g, y] = coef * (val(g + 1, y) - val(g - 1, y))
                    b[q, 1, l0 + g, y] = coef * (val(g, y + 1) - val(g, y - 1))
                    b[q, 2, l0 + g, y] = coef * (
                        jnp.where(last_z, 0.0, right(x)) - jnp.where(first_z, 0.0, left(x))
                    )
            return a

        lax.fori_loop(0, (LT - 4) // 4, grad, 0)
        mo = first_pass(q, e_ops, b, we, 3, EN)
        halo_pass(q, e_ops, b, we, 3, 1, 1)
        (m3,) = second_pass(q, e_ops, we, 3, EN)
        red_start(base + NB + q, (*mo, m3))

    def displace_far(q):
        halo_pass(q, e_ops, b, we, 3, K - 3, 2, 1)

    def again(q, base, idx):
        z0, z1 = weights(red_wait(base + NB + q))
        y0, y1 = wts[q, 0], wts[q, 1]

        def resid(l0, n, a):
            def flow(k):
                def make(g, y):
                    l = l0 + g
                    return hb[l, y] * (z0 * b[q, k, l, y] + z1 * we[q, k, l, y])

                return Made(make)

            fx, fy, fz = flow(0), flow(1), flow(2)
            for y in range(yh):
                for g in range(n):
                    l = l0 + g
                    tz = fz(g, y)
                    div = fx(g - 1, y) - fx(g + 1, y)
                    div = div + (fy(g, y - 1) - fy(g, y + 1))
                    div = div + (
                        jnp.where(first_z, 0.0, left(tz)) - jnp.where(last_z, 0.0, right(tz))
                    )
                    image = y0 * w[q, l, y] + y1 * v[q, l, y]
                    r2[q, l, y] = f[q, l, y] - div + st[l, y] * p1[q, l, y] - image
            return a

        own_loop(4, resid, 0)
        halo_loop(2, 2, resid)
        mo = first_pass(q, p_ops, r2, w2, None, PN)

        @pl.when(idx == 0)
        def _():
            strip_do(r_strip(q), start=True)

        halo_pass(q, p_ops, r2, w2, None, 1, 1)
        (m3,) = second_pass(q, p_ops, w2, None, PN)
        red_start(base + 2 * NB + q, (*mo, m3))

    def again_far(q):
        strip_do(r_strip(q), recv=True, sent=True)
        halo_pass(q, p_ops, r2, w2, None, 2, 1, 1)

    def close(q, base, idx):
        x0, x1 = weights(red_wait(base + 2 * NB + q))

        def total(l, y):
            return p1[q, l, y] + x0 * r2[q, l, y] + x1 * w2[q, l, y]

        @pl.when(idx == 0)
        def _():
            def update(i, a):
                for g in range(2):
                    l = O - NEAR + 2 * i + g
                    for y in range(yh):
                        f[q, l, y] = total(l, y) * row_of(c_obs, l, y)
                return a

            lax.fori_loop(0, NL // 2 + NEAR, update, 0)
            strip_do(f_strip(q), start=True)

        @pl.when(idx > 0)
        def _():
            def finish(i, a):
                for g in range(2):
                    l = 2 * i + g
                    for y in range(yh):
                        ybuf[q, l, y] = total(O + l, y) * row_of(c_bs, O + l, y)
                return a

            lax.fori_loop(0, NL // 2, finish, 0)
            for l in range(per):
                for j in range(1, nq):
                    gram_copy(q, l, lax.rem(me + j, nq), me).start()

    def solve(idx, a):
        base = idx * NB * 3
        with jax.named_scope("g_P1"):
            each(begin, base)

        @pl.when(idx == 0)
        def _():
            far_layers()

        with jax.named_scope("g_far"):
            each(begin_far, idx)
        with jax.named_scope("h_E"):
            each(displace, base)
        with jax.named_scope("h_Efar"):
            each(displace_far)
        with jax.named_scope("i_P2"):
            each(again, base, idx)

        with jax.named_scope("j_far"):

            @pl.when(idx == 0)
            def _():
                each(again_far)
                wait_halo((6,))

        with jax.named_scope("k_close"):
            each(close, base, idx)
        return a

    phase()
    lax.fori_loop(0, 2, solve, 0)

    phase("l_unpack")
    hflat = hraw.reshape(NDEV * OWN * ny, LANES)
    oflat = hess.reshape(2 * NDEV * OWN * ny, LANES)

    def unpack(dst, base, at):
        def layer(i, a):
            for q in range(NB):
                for y in range(yh):
                    val = ybuf[q, at + i, y]
                    for h in range(HV):
                        dst[
                            pl.ds(
                                base + (q * ND * OWN + i) * ny + h * yh + y,
                                ND,
                                stride=OWN * ny,
                            ),
                            :,
                        ] = val[h * ND : (h + 1) * ND]
            return a

        lax.fori_loop(0, OWN, layer, 0)

    unpack(hflat, 0, OWN * (1 - c))

    def own_gram(i, a):
        for q in range(NB):
            for y in range(yh):
                grecv[me, q, i, y] = ybuf[q, per * me + i, y]
        return a

    lax.fori_loop(0, per, own_gram, 0)
    swap = remote(hraw, hess.at[pl.ds(NDEV * c, NDEV)], sem_h.at[0], sem_h.at[1], partner, d)
    swap.start()
    unpack(oflat, NDEV * c * OWN * ny, OWN * c)

    width = nq * NB * SUB
    g_all = jnp.zeros((width, width), F32)
    for l in range(per):
        phase("m_gramwait")
        for q in range(NB):
            for j in range(1, nq):
                slot = lax.rem(me + j, nq)
                gram_copy(q, l, slot, slot).wait_recv()
        phase("m_gramdot")
        for y in range(0, yh, 2):
            z = jnp.concatenate(
                [grecv[:, :, l, y + i].reshape(width, LANES) for i in range(2)], axis=1
            )
            g_all = g_all + lax.dot_general(
                z,
                z,
                (((1,), (1,)), ((), ())),
                precision=lax.Precision.HIGHEST,
                preferred_element_type=F32,
            )
    phase("m_fold")
    ndir = nq * NDEV
    fold = jnp.zeros((ndir, LANES), F32)
    for h in range(HV):
        ri = lax.broadcasted_iota(jnp.int32, (ndir, width), 0)
        ci = lax.broadcasted_iota(jnp.int32, (ndir, width), 1)
        left_sel = jnp.where(ci == (ri // ND) * SUB + h * ND + lax.rem(ri, ND), 1.0, 0.0)
        rj = lax.broadcasted_iota(jnp.int32, (width, LANES), 0)
        cj = lax.broadcasted_iota(jnp.int32, (width, LANES), 1)
        right_sel = jnp.where(
            jnp.logical_and(rj == (cj // ND) * SUB + h * ND + lax.rem(cj, ND), cj < ndir),
            1.0,
            0.0,
        )
        mid = jnp.dot(
            left_sel, g_all, precision=lax.Precision.HIGHEST, preferred_element_type=F32
        )
        fold = fold + jnp.dot(
            mid, right_sel, precision=lax.Precision.HIGHEST, preferred_element_type=F32
        )
    packed = fold[0:SUB]
    for k in range(1, ndir // SUB):
        packed = packed + pltpu.roll(fold[k * SUB : (k + 1) * SUB], ndir * k, 1)

    phase("n_ga")
    ga_src[...] = packed
    ga_buf[s] = packed

    def ga_copy(j, slot):
        peer = lax.rem(s + j, ns)
        return remote(
            ga_src, ga_buf.at[slot], sem_ga_send.at[j], sem_ga.at[slot], peer * 2 + c, d
        )

    for j in range(1, ns):
        ga_copy(j, s).start()
    for j in range(1, ns):
        ga_copy(j, lax.rem(s + j, ns)).wait_recv()
    total = ga_buf[0]
    for j in range(1, ns):
        total = total + ga_buf[j]
    phase("n_gb")
    gb_src[...] = total
    gb_buf[me] = total

    def gb_copy(j, slot):
        q = lax.rem(me + j, nq)
        return remote(
            gb_src,
            gb_buf.at[slot],
            sem_gb_send.at[j],
            sem_gb.at[slot],
            s * 2 + lax.rem(q, 2),
            q // 2,
        )

    for j in range(1, nq):
        gb_copy(j, me).start()
    for j in range(1, nq):
        gb_copy(j, lax.rem(me + j, nq)).wait_recv()
    total = gb_buf[0]
    for j in range(1, nq):
        total = total + gb_buf[j]
    total = total * (1.0 / cells)
    for k in range(ndir // SUB):
        row = total if k == 0 else pltpu.roll(total, LANES - ndir * k, 1)
        gram[k * SUB : (k + 1) * SUB] = row

    phase("o_drain")
    swap.wait_recv()
    swap.wait_send()
    for cp in part_copies():
        cp.wait_send()

    @pl.when(has_cross)
    def _():
        for cp in cross_copies():
            cp.wait_send()

    def red_sent(r, a):
        for j in range(1, ns):
            red_copy(r, j, s).wait_send()
        return a

    lax.fori_loop(0, NRED, red_sent, 0)

    def batch_sent(q, a):
        strip_do(f_strip(q), sent=True)
        for l in range(per):
            for j in range(1, nq):
                gram_copy(q, l, lax.rem(me + j, nq), me).wait_send()
        return a

    lax.fori_loop(0, NB, batch_sent, 0)
    for j in range(1, ns):
        ga_copy(j, s).wait_send()
    for j in range(1, nq):
        gb_copy(j, me).wait_send()
    phase()


PN = 4
EN = 2


def last_kernel(gram, h_in, r_out, h_out, buf, sems):
    into = pltpu.make_async_copy(h_in, buf, sems.at[0])
    into.start()
    n = r_out.shape[0]
    lane = lax.broadcasted_iota(jnp.int32, (1, LANES), 1)
    a = gram[...]
    into.wait()
    out = pltpu.make_async_copy(buf, h_out, sems.at[1])
    out.start()
    for j in range(n):
        col = jnp.broadcast_to(a[:, j : j + 1], (n, LANES))
        inv = 1.0 / jnp.sqrt(col[j : j + 1])
        row = a[j : j + 1] * inv
        r_out[j : j + 1] = jnp.where(lane >= j, row, 0.0)[:, 0:n]
        if j + 1 < n:
            a = a - (col * inv) * row
    out.wait()


def solution(mesh):
    ns = mesh.shape["tile"] // 2
    nd = mesh.shape["dir"]
    nq = 2 * nd
    ndir = nq * NDEV

    def body(probes, bs, obs, perm, mat, storage, alpha, bulk, shear):
        ny, nz = probes.shape[2:]
        yh = ny // HV
        per = NL // nq
        cells = OWN * 2 * ns * ny * nz
        vm = pl.BlockSpec(memory_space=pltpu.VMEM)
        sm = pl.BlockSpec(memory_space=pltpu.SMEM)
        anywhere = pl.BlockSpec(memory_space=pl.ANY)

        def compact(kind=F32):
            return pltpu.VMEM((LT, ny, nz), kind)

        def wide(rows=yh, pre=()):
            return pltpu.VMEM((*pre, LT, rows, SUB, nz), F32)

        dma = pltpu.SemaphoreType.DMA
        field = wide(pre=(NB,))
        scratch = [
            pltpu.VMEM(probes.shape, F32),
            pltpu.VMEM((NDEV, LT, ny, nz), F32),
            compact(),
            compact(),
            compact(),
            compact(jnp.int32),
            compact(),
            compact(),
            compact(),
            compact(),
            pltpu.VMEM((10, ny + SUB, nz), F32),
            *[wide(), wide(), wide(yh + 1), wide(), wide()] * 2,
            wide(),
            wide(),
            field,
            field,
            field,
            field,
            wide(pre=(NB, 3)),
            wide(pre=(NB, 3)),
            field,
            field,
            pltpu.VMEM((NB, NL, yh, SUB, nz), F32),
            pltpu.VMEM((NDEV, OWN, ny, nz), F32),
            pltpu.VMEM((nq, NB, per, yh, SUB, nz), F32),
            pltpu.VMEM((NB, 2, SUB, nz), F32),
            pltpu.VMEM((NRED, 1, nz), F32),
            pltpu.VMEM((NRED, ns, 1, nz), F32),
            pltpu.VMEM((SUB, nz), F32),
            pltpu.VMEM((ns, SUB, nz), F32),
            pltpu.VMEM((SUB, nz), F32),
            pltpu.VMEM((nq, SUB, nz), F32),
            dma((5 + 14,)),
            dma((5,)),
            dma((2, 7)),
            dma((NRED, ns)),
            dma((NRED, ns)),
            dma((ns,)),
            dma((ns,)),
            dma((nq,)),
            dma((nq,)),
            dma((NB, per, nq)),
            dma((NB, per, nq)),
            dma((2,)),
            dma((NB, 2)),
            dma((NB, 2)),
            dma((NB, 2)),
            dma((NB, 2)),
        ]
        hess, gram = pl.pallas_call(
            functools.partial(kernel, ns, nd, cells),
            out_shape=(
                jax.ShapeDtypeStruct(probes.shape, F32),
                jax.ShapeDtypeStruct((ndir, nz), F32),
            ),
            in_specs=[vm] * 5 + [sm] * 4,
            out_specs=(vm, vm),
            scratch_shapes=scratch,
            compiler_params=pltpu.CompilerParams(
                collective_id=0, has_side_effects=True, vmem_limit_bytes=67043328
            ),
            name="solve",
        )(probes, bs, obs, perm, mat, storage, alpha, bulk, shear)
        r_factor, hess = pl.pallas_call(
            last_kernel,
            out_shape=(
                jax.ShapeDtypeStruct((ndir, ndir), F32),
                jax.ShapeDtypeStruct(probes.shape, F32),
            ),
            in_specs=[vm, anywhere],
            out_specs=(vm, anywhere),
            scratch_shapes=[pltpu.VMEM(probes.shape, F32), dma((2,))],
            name="factor",
        )(gram, hess)
        return hess, r_factor

    return jax.shard_map(
        body,
        mesh=mesh,
        in_specs=(
            P("dir", "tile", None, None),
            P("tile", None, None),
            P("tile", None, None),
            P("tile", None, None),
            P("tile", None, None),
            P(),
            P(),
            P(),
            P(),
        ),
        out_specs=(P("dir", "tile", None, None), P()),
        check_vma=False,
    )
```

time: 139 us -> 112 us (0.81)
  Pallas kernels: 129 us -> 110 us
  other arithmetic: 4.25 us -> 0 us
  local copies, waits for them, and re-layouts: 3.83 us -> 0 us
    pallas_call x1, Pallas kernels: 129 us -> 104 us  [body(): pl.pallas_call(functools.partial(kernel, ns, nd, cells), out_shape=(jax.S...]
    pallas_call x0 -> x1, Pallas kernels: none -> 5.54 us  [body(): pl.pallas_call(last_kernel, out_shape=(jax.ShapeDtypeStruct((ndir, ndir),...]
    another operation x3 -> x0, other arithmetic: 3.6 us -> none  [body(): r_factor = jnp.linalg.cholesky(gram[:, :nq * ND]).T]
    unnamed x2 -> x0, local copies, waits for them, and re-layouts: 2.94 us -> none
where the time goes in v2:
time: 112 us; the launch traced here: 110 us
  Pallas kernels  110 us (98%)
    pallas_call x1, Pallas kernels, body(): pl.pallas_call(functools.partial(kernel, ns, nd, cells), out_shape=(jax.S...  104 us
    pallas_call x1, Pallas kernels, body(): pl.pallas_call(last_kernel, out_shape=(jax.ShapeDtypeStruct((ndir, ndir),...  5.54 us

profile of v2, /device:TPU:0, one launch (start us, length us, event | category | flops | bytes accessed | tf_op | source)
XLA Modules:
  0.0 110.4 jit_solution(7569293276214831502)
XLA Ops:
  0.6 104.2 %solve.1 = (f32[8,8,32,128]{3,2,1,0:T(8,128)}, f32[32,128]{1,0:T(8,128)}) custom-call(f32[8,8,32,128]{3,2,1,0:T(8,128)} %probes.1, f32[8,32,128]{2,1,0:T(8,128)} %bs_in.1, f32[8,32,128]{2,1,0:T(8,128)} %obs_in.1, f32[8,32,128]{2,1,0:T(8,128)} %perm_in.1, s32[8,32,128]{2,1,0:T(8,128)} %mat_in.1, f32[8]{0:T(128)} %t_storage.1, f32[8]{0:T(128)} %t_alpha.1, ...), custom_call_target="tpu_custom_call" | custom-call | tf_op jit(solution)/shard_map/solve/pallas_call | solution.py:1079
  104.9 5.5 %factor.1 = (f32[32,32]{1,0:T(8,128)}, f32[8,8,32,128]{3,2,1,0:T(8,128)}) custom-call(f32[32,128]{1,0:T(8,128)} %get-tuple-element.6.gram, f32[8,8,32,128]{3,2,1,0:T(8,128)} %get-tuple-element.7.h_in), custom_call_target="tpu_custom_call" | custom-call | tf_op jit(solution)/shard_map/factor/pallas_call | solution.py:1093

commit v3 on v2

--- a/solution.py
+++ b/solution.py
@@ -30,17 +30,22 @@
     ns,
     nd,
     cells,
-    probes,
-    bs_in,
-    obs_in,
-    perm_in,
-    mat_in,
+    probes_at,
+    bs_at,
+    obs_at,
+    perm_at,
+    mat_at,
     t_storage,
     t_alpha,
     t_bulk,
     t_shear,
     hess,
     gram,
+    probes,
+    bs_in,
+    obs_in,
+    perm_in,
+    mat_in,
     fraw,
     praw,
     c_bs,
@@ -74,6 +79,8 @@
     w2,
     ybuf,
     hraw,
+    hin,
+    hout,
     grecv,
     wts,
     red_src,
@@ -87,9 +94,7 @@
     sem_halo,
     sem_red_send,
     sem_red,
-    sem_ga_send,
     sem_ga,
-    sem_gb_send,
     sem_gb,
     sem_g_send,
     sem_g,
@@ -98,6 +103,8 @@
     sem_f,
     sem_r_send,
     sem_r,
+    sem_in,
+    sem_out,
 ):
     scope = []
 
@@ -138,22 +145,25 @@
     def _():
         greet(cross * 2 + (1 - c), d)
 
+    loads = [
+        pltpu.make_async_copy(src, dst, sem_in.at[i])
+        for i, (src, dst) in enumerate(
+            (
+                (mat_at, mat_in),
+                (bs_at, bs_in),
+                (probes_at, probes),
+                (perm_at, perm_in),
+                (obs_at, obs_in),
+            )
+        )
+    ]
+    for cp in loads:
+        cp.start()
+
     own_at = O + OWN * c
     zero8 = jnp.zeros((SUB, LANES), F32)
     zc = jnp.zeros((ny, LANES), F32)
     zi = jnp.zeros((ny, LANES), jnp.int32)
-
-    def products(l, a):
-        sens = bs_in[l]
-        for dd in range(2 * NDEV):
-            fraw[dd, l] = probes[dd, l] * sens
-        c_bs[own_at + l] = sens
-        c_obs[own_at + l] = obs_in[l]
-        c_perm[own_at + l] = perm_in[l]
-        c_mat[own_at + l] = mat_in[l]
-        return a
-
-    lax.fori_loop(0, OWN, products, 0)
 
     def zero_side(lo):
         def layer(i, carry):
@@ -182,6 +192,21 @@
     @pl.when(jnp.logical_not(has_high))
     def _():
         zero_side(E)
+
+    for cp in loads:
+        cp.wait()
+
+    def products(l, a):
+        sens = bs_in[l]
+        for dd in range(2 * NDEV):
+            fraw[dd, l] = probes[dd, l] * sens
+        c_bs[own_at + l] = sens
+        c_obs[own_at + l] = obs_in[l]
+        c_perm[own_at + l] = perm_in[l]
+        c_mat[own_at + l] = mat_in[l]
+        return a
+
+    lax.fori_loop(0, OWN, products, 0)
 
     lane = lax.broadcasted_iota(jnp.int32, (SUB, LANES), 1)
     sub = lax.broadcasted_iota(jnp.int32, (SUB, LANES), 0)
@@ -550,11 +575,17 @@
         return remote(
             red_src.at[r],
             red_buf.at[r, slot],
-            sem_red_send.at[r, j],
-            sem_red.at[r, slot],
+            sem_red_send.at[r],
+            sem_red.at[r],
             peer * 2 + c,
             d,
         )
+
+    def whole(block, ssem, rsem):
+        return remote(block, block, ssem, rsem, partner, d)
+
+    def red_all(r):
+        return whole(red_buf.at[r, pl.ds(0, ns - 1)], sem_red_send.at[r], sem_red.at[r])
 
     def red_start(r, moments):
         row = jnp.zeros((SUB, LANES), F32)
@@ -570,8 +601,7 @@
             red_copy(r, j, s).start()
 
     def red_wait(r):
-        for j in range(1, ns):
-            red_copy(r, j, lax.rem(s + j, ns)).wait_recv()
+        red_all(r).wait_recv()
         total = red_buf[r, 0]
         for j in range(1, ns):
             total = total + red_buf[r, j]
@@ -651,10 +681,15 @@
         return remote(
             ybuf.at[bt, per * q + l],
             grecv.at[slot, bt, l],
-            sem_g_send.at[bt, l, q],
-            sem_g.at[bt, l, slot],
+            sem_g_send.at[bt, l],
+            sem_g.at[bt, l],
             s * 2 + lax.rem(q, 2),
             q // 2,
+        )
+
+    def gram_all(bt, l):
+        return whole(
+            grecv.at[pl.ds(0, nq - 1), bt, l], sem_g_send.at[bt, l], sem_g.at[bt, l]
         )
 
     def each(stage, *args):
@@ -825,28 +860,20 @@
     lax.fori_loop(0, 2, solve, 0)
 
     phase("l_unpack")
-    hflat = hraw.reshape(NDEV * OWN * ny, LANES)
-    oflat = hess.reshape(2 * NDEV * OWN * ny, LANES)
-
-    def unpack(dst, base, at):
+
+    def unpack(dst, at):
+        flat = dst.reshape(NDEV * OWN * ny, LANES)
+
         def layer(i, a):
             for q in range(NB):
                 for y in range(yh):
                     val = ybuf[q, at + i, y]
                     for h in range(HV):
-                        dst[
-                            pl.ds(
-                                base + (q * ND * OWN + i) * ny + h * yh + y,
-                                ND,
-                                stride=OWN * ny,
-                            ),
-                            :,
-                        ] = val[h * ND : (h + 1) * ND]
+                        row = (q * ND * OWN + i) * ny + h * yh + y
+                        flat[pl.ds(row, ND, stride=OWN * ny), :] = val[h * ND : (h + 1) * ND]
             return a
 
         lax.fori_loop(0, OWN, layer, 0)
-
-    unpack(hflat, 0, OWN * (1 - c))
 
     def own_gram(i, a):
         for q in range(NB):
@@ -854,19 +881,24 @@
                 grecv[me, q, i, y] = ybuf[q, per * me + i, y]
         return a
 
+    unpack(hraw, OWN * (1 - c))
+    unpack(hout, OWN * c)
+    swap = remote(hraw, hin, sem_h.at[0], sem_h.at[1], partner, d)
+    swap.start()
     lax.fori_loop(0, per, own_gram, 0)
-    swap = remote(hraw, hess.at[pl.ds(NDEV * c, NDEV)], sem_h.at[0], sem_h.at[1], partner, d)
-    swap.start()
-    unpack(oflat, NDEV * c * OWN * ny, OWN * c)
+    put = pltpu.make_async_copy(hout, hess.at[pl.ds(NDEV * c, NDEV)], sem_out.at[0])
+    put.start()
+    put_in = pltpu.make_async_copy(hin, hess.at[pl.ds(NDEV * (1 - c), NDEV)], sem_out.at[1])
 
     width = nq * NB * SUB
     g_all = jnp.zeros((width, width), F32)
     for l in range(per):
         phase("m_gramwait")
         for q in range(NB):
-            for j in range(1, nq):
-                slot = lax.rem(me + j, nq)
-                gram_copy(q, l, slot, slot).wait_recv()
+            gram_all(q, l).wait_recv()
+        if l == 0:
+            swap.wait_recv()
+            put_in.start()
         phase("m_gramdot")
         for y in range(0, yh, 2):
             z = jnp.concatenate(
@@ -910,13 +942,13 @@
     def ga_copy(j, slot):
         peer = lax.rem(s + j, ns)
         return remote(
-            ga_src, ga_buf.at[slot], sem_ga_send.at[j], sem_ga.at[slot], peer * 2 + c, d
+            ga_src, ga_buf.at[slot], sem_ga.at[0], sem_ga.at[1], peer * 2 + c, d
         )
 
     for j in range(1, ns):
         ga_copy(j, s).start()
-    for j in range(1, ns):
-        ga_copy(j, lax.rem(s + j, ns)).wait_recv()
+    ga_all = whole(ga_buf.at[pl.ds(0, ns - 1)], sem_ga.at[0], sem_ga.at[1])
+    ga_all.wait_recv()
     total = ga_buf[0]
     for j in range(1, ns):
         total = total + ga_buf[j]
@@ -929,16 +961,16 @@
         return remote(
             gb_src,
             gb_buf.at[slot],
-            sem_gb_send.at[j],
-            sem_gb.at[slot],
+            sem_gb.at[0],
+            sem_gb.at[1],
             s * 2 + lax.rem(q, 2),
             q // 2,
         )
 
     for j in range(1, nq):
         gb_copy(j, me).start()
-    for j in range(1, nq):
-        gb_copy(j, lax.rem(me + j, nq)).wait_recv()
+    gb_all = whole(gb_buf.at[pl.ds(0, nq - 1)], sem_gb.at[0], sem_gb.at[1])
+    gb_all.wait_recv()
     total = gb_buf[0]
     for j in range(1, nq):
         total = total + gb_buf[j]
@@ -948,8 +980,9 @@
         gram[k * SUB : (k + 1) * SUB] = row
 
     phase("o_drain")
-    swap.wait_recv()
     swap.wait_send()
+    put.wait()
+    put_in.wait()
     for cp in part_copies():
         cp.wait_send()
 
@@ -959,8 +992,7 @@
             cp.wait_send()
 
     def red_sent(r, a):
-        for j in range(1, ns):
-            red_copy(r, j, s).wait_send()
+        red_all(r).wait_send()
         return a
 
     lax.fori_loop(0, NRED, red_sent, 0)
@@ -968,39 +1000,56 @@
     def batch_sent(q, a):
         strip_do(f_strip(q), sent=True)
         for l in range(per):
-            for j in range(1, nq):
-                gram_copy(q, l, lax.rem(me + j, nq), me).wait_send()
+            gram_all(q, l).wait_send()
         return a
 
     lax.fori_loop(0, NB, batch_sent, 0)
-    for j in range(1, ns):
-        ga_copy(j, s).wait_send()
-    for j in range(1, nq):
-        gb_copy(j, me).wait_send()
+    ga_all.wait_send()
+    gb_all.wait_send()
     phase()
 
 
 PN = 4
-EN = 2
+EN = 4
+
+
+AHEAD = 3
 
 
 def last_kernel(gram, h_in, r_out, h_out, buf, sems):
-    into = pltpu.make_async_copy(h_in, buf, sems.at[0])
-    into.start()
+    parts = h_in.shape[0] // 2
+    at = [pl.ds(2 * i, 2) for i in range(parts)]
+    into = [pltpu.make_async_copy(h_in.at[p], buf.at[p], sems.at[0, i]) for i, p in enumerate(at)]
+    out = [pltpu.make_async_copy(buf.at[p], h_out.at[p], sems.at[1, i]) for i, p in enumerate(at)]
+    for cp in into:
+        cp.start()
     n = r_out.shape[0]
     lane = lax.broadcasted_iota(jnp.int32, (1, LANES), 1)
     a = gram[...]
-    into.wait()
-    out = pltpu.make_async_copy(buf, h_out, sems.at[1])
-    out.start()
+
+    def wide(x, j):
+        return jnp.broadcast_to(x[:, j : j + 1], (n, LANES))
+
+    cols = {j: (wide(a, j), 0) for j in range(AHEAD)}
+    done = []
     for j in range(n):
-        col = jnp.broadcast_to(a[:, j : j + 1], (n, LANES))
-        inv = 1.0 / jnp.sqrt(col[j : j + 1])
+        col, first = cols.pop(j)
+        for m in range(first, j):
+            col = col - done[m] * done[m][j : j + 1]
+        inv = lax.rsqrt(col[j : j + 1])
+        inv = inv * (1.5 - 0.5 * col[j : j + 1] * inv * inv)
+        col = col * inv
+        done.append(col)
         row = a[j : j + 1] * inv
         r_out[j : j + 1] = jnp.where(lane >= j, row, 0.0)[:, 0:n]
-        if j + 1 < n:
-            a = a - (col * inv) * row
-    out.wait()
+        a = a - col * row
+        if j + AHEAD < n:
+            cols[j + AHEAD] = (wide(a, j + AHEAD), j + 1)
+        if j % 4 == 3 and j // 4 < parts:
+            into[j // 4].wait()
+            out[j // 4].start()
+    for cp in out:
+        cp.wait()
 
 
 def solution(mesh):
@@ -1027,6 +1076,8 @@
         dma = pltpu.SemaphoreType.DMA
         field = wide(pre=(NB,))
         scratch = [
+            pltpu.VMEM(probes.shape, F32),
+            *[pltpu.VMEM(x.shape, x.dtype) for x in (bs, obs, perm, mat)],
             pltpu.VMEM(probes.shape, F32),
             pltpu.VMEM((NDEV, LT, ny, nz), F32),
             compact(),
@@ -1050,7 +1101,7 @@
             field,
             field,
             pltpu.VMEM((NB, NL, yh, SUB, nz), F32),
-            pltpu.VMEM((NDEV, OWN, ny, nz), F32),
+            *[pltpu.VMEM((NDEV, OWN, ny, nz), F32)] * 3,
             pltpu.VMEM((nq, NB, per, yh, SUB, nz), F32),
             pltpu.VMEM((NB, 2, SUB, nz), F32),
             pltpu.VMEM((NRED, 1, nz), F32),
@@ -1062,19 +1113,19 @@
             dma((5 + 14,)),
             dma((5,)),
             dma((2, 7)),
-            dma((NRED, ns)),
-            dma((NRED, ns)),
-            dma((ns,)),
-            dma((ns,)),
-            dma((nq,)),
-            dma((nq,)),
-            dma((NB, per, nq)),
-            dma((NB, per, nq)),
+            dma((NRED,)),
+            dma((NRED,)),
+            dma((2,)),
+            dma((2,)),
+            dma((NB, per)),
+            dma((NB, per)),
             dma((2,)),
             dma((NB, 2)),
             dma((NB, 2)),
             dma((NB, 2)),
             dma((NB, 2)),
+            dma((5,)),
+            dma((2,)),
         ]
         hess, gram = pl.pallas_call(
             functools.partial(kernel, ns, nd, cells),
@@ -1082,8 +1133,8 @@
                 jax.ShapeDtypeStruct(probes.shape, F32),
                 jax.ShapeDtypeStruct((ndir, nz), F32),
             ),
-            in_specs=[vm] * 5 + [sm] * 4,
-            out_specs=(vm, vm),
+            in_specs=[anywhere] * 5 + [sm] * 4,
+            out_specs=(anywhere, vm),
             scratch_shapes=scratch,
             compiler_params=pltpu.CompilerParams(
                 collective_id=0, has_side_effects=True, vmem_limit_bytes=67043328
@@ -1098,7 +1149,7 @@
             ),
             in_specs=[vm, anywhere],
             out_specs=(vm, anywhere),
-            scratch_shapes=[pltpu.VMEM(probes.shape, F32), dma((2,))],
+            scratch_shapes=[pltpu.VMEM(probes.shape, F32), dma((2, probes.shape[0] // 2))],
             name="factor",
         )(gram, hess)
         return hess, r_factor

time: 112 us -> 102 us (0.911)
  Pallas kernels: 110 us -> 101 us
    pallas_call x1, Pallas kernels: 104 us -> 97.1 us  [body(): pl.pallas_call(functools.partial(kernel, ns, nd, cells), out_shape=(jax.S...]
    pallas_call x1, Pallas kernels: 5.54 us -> 3.56 us  [body(): pl.pallas_call(last_kernel, out_shape=(jax.ShapeDtypeStruct((ndir, ndir),...]
where the time goes in v3:
time: 102 us; the launch traced here: 101 us
  Pallas kernels  101 us (99%)
    pallas_call x1, Pallas kernels, body(): pl.pallas_call(functools.partial(kernel, ns, nd, cells), out_shape=(jax.S...  97.1 us
    pallas_call x1, Pallas kernels, body(): pl.pallas_call(last_kernel, out_shape=(jax.ShapeDtypeStruct((ndir, ndir),...  3.56 us

profile of v3, /device:TPU:0, one launch (start us, length us, event | category | flops | bytes accessed | tf_op | source)
XLA Modules:
  0.0 101.3 jit_solution(9069004041183417193)
XLA Ops:
  0.6 97.1 %solve.1 = (f32[8,8,32,128]{3,2,1,0:T(8,128)}, f32[32,128]{1,0:T(8,128)}) custom-call(f32[8,8,32,128]{3,2,1,0:T(8,128)} %probes_at.1, f32[8,32,128]{2,1,0:T(8,128)} %bs_at.1, f32[8,32,128]{2,1,0:T(8,128)} %obs_at.1, f32[8,32,128]{2,1,0:T(8,128)} %perm_at.1, s32[8,32,128]{2,1,0:T(8,128)} %mat_at.1, f32[8]{0:T(128)} %t_storage.1, f32[8]{0:T(128)} %t_alpha.1, ...), custom_call_target="tpu_custom_call" | custom-call | tf_op jit(solution)/shard_map/solve/pallas_call | solution.py:1130
  97.7 3.6 %factor.1 = (f32[32,32]{1,0:T(8,128)}, f32[8,8,32,128]{3,2,1,0:T(8,128)}) custom-call(f32[32,128]{1,0:T(8,128)} %get-tuple-element.6.gram, f32[8,8,32,128]{3,2,1,0:T(8,128)} %get-tuple-element.7.h_in), custom_call_target="tpu_custom_call" | custom-call | tf_op jit(solution)/shard_map/factor/pallas_call | solution.py:1144

commit v4 on v3

--- a/solution.py
+++ b/solution.py
@@ -18,8 +18,8 @@
 O = K
 E = K + NL
 LT = NL + 2 * K
-NB = 2
-HV = 4
+NB = 4
+HV = 8
 ND = SUB // HV
 NDEV = NB * ND
 NEAR = 2
@@ -329,15 +329,8 @@
             for cp in halo_copies(1, s, (0, E), (NEAR, E + NEAR), (0,), only):
                 cp.wait_recv()
 
-    def wide_row(read, y):
-        val = jnp.broadcast_to(read(y), (SUB, LANES))
-        for h in range(1, HV):
-            more = jnp.broadcast_to(read(y + h * yh), (SUB, LANES))
-            val = jnp.where(part_of >= h, more, val)
-        return val
-
     def row_of(ref, l, y):
-        return wide_row(lambda y: ref[l, pl.ds(y, 1), :], y)
+        return ref[l, pl.ds(y, HV, stride=yh), :]
 
     def spread_rows(dst, l, idx, rows=None):
         for y in range(yh if rows is None else rows):
@@ -403,14 +396,8 @@
             l = lo + i
             for q in range(NB):
                 for y in range(yh):
-                    base = ((first + q * ND) * layers + (l - shift)) * ny + y
-                    f[q, l, y] = jnp.concatenate(
-                        [
-                            flat[pl.ds(base + h * yh, ND, stride=layers * ny), :]
-                            for h in range(HV)
-                        ],
-                        axis=0,
-                    )
+                    row = ((first + q) * layers + (l - shift)) * ny + y
+                    f[q, l, y] = flat[pl.ds(row, HV, stride=yh), :]
             return carry
 
         lax.fori_loop(0, n, layer, 0)
@@ -419,31 +406,36 @@
     faces(own_at + 1, OWN - 2)
     source(own_at, OWN, fraw, NDEV * c, own_at, OWN)
     phase("d_wait_part")
-    for cp in part_copies():
-        cp.wait_recv()
+    parts = part_copies()
+    for i in (0, 1):
+        parts[i].wait_recv()
     phase("d_other")
     other_at = O + OWN * (1 - c)
     tables(other_at, OWN)
     faces(jnp.where(c == 0, O + OWN - 1, O + 1), OWN)
+    for i in (2, 3, 4):
+        parts[i].wait_recv()
     source(other_at, OWN)
     phase("d_wait_near")
-    wait_halo((0, 1, 2))
-    phase("d_near")
+    wait_halo((0, 1))
     tables(O - NEAR, NEAR)
     tables(E, NEAR)
     faces(O - 1, 2)
     faces(E - 1, 2)
     x_faces(O - 2)
+    phase("d_near")
+    wait_halo((2,))
     source(O - NEAR, NEAR)
     source(E, NEAR)
 
     def far_layers():
-        wait_halo((3, 4, 5))
+        wait_halo((3, 4))
         tables(0, K - NEAR)
         tables(E + NEAR, K - NEAR)
         faces(1, K - NEAR)
         faces(E + 1, K - NEAR)
         x_faces(0)
+        wait_halo((5,))
         source(0, K - NEAR)
         source(E + NEAR, K - NEAR)
 
@@ -508,16 +500,24 @@
     def own_loop(n, body, init):
         return lax.fori_loop(0, NL // n, lambda i, a: body(O + i * n, n, a), init)
 
-    def halo_loop(k, n, body, far=0):
-        trips = (k - far) // n
-
-        @pl.when(has_low)
+    def both_halos(k, far, body, outs):
+        n = k - far
+        body(O - k, n)
+        body(E + far, n)
+
+        def clear(at):
+            for ref, pre in outs:
+                for g in range(n):
+                    for y in range(yh):
+                        ref[(*pre, at + g, y)] = zero8
+
+        @pl.when(jnp.logical_not(has_low))
         def _():
-            lax.fori_loop(0, trips, lambda i, a: body(O - k + i * n, n, a), 0)
-
-        @pl.when(has_high)
+            clear(O - k)
+
+        @pl.when(jnp.logical_not(has_high))
         def _():
-            lax.fori_loop(0, trips, lambda i, a: body(E + far + i * n, n, a), 0)
+            clear(E + far)
 
     def pres(q, comps):
         return [(q,)] if comps is None else [(q, k) for k in range(comps)]
@@ -539,17 +539,16 @@
 
         return own_loop(n, body, (zero8,) * 3)
 
-    def halo_pass(q, ops, src, dst, comps, k, n, far=0):
+    def halo_pass(q, ops, src, dst, comps, k, far=0):
         pre = pres(q, comps)
 
-        def body(l0, n, acc):
+        def body(l0, n):
             def emit(kk, g, y, x, out):
                 dst[(*pre[kk], l0 + g, y)] = out
 
             group(ops, [Rows(src, l0, kk) for kk in pre], l0, n, emit)
-            return acc
-
-        halo_loop(k, n, body, far)
+
+        both_halos(k, far, body, [(dst, p) for p in pre])
 
     def second_pass(q, ops, src, comps, n, dst=None):
         pre = pres(q, comps)
@@ -566,9 +565,6 @@
             return tuple(acc)
 
         return own_loop(n, body, (zero8,))
-
-    GAP = LANES // SUB
-    packed_at = lane // GAP == sub
 
     def red_copy(r, j, slot):
         peer = lax.rem(s + j, ns)
@@ -588,13 +584,7 @@
         return whole(red_buf.at[r, pl.ds(0, ns - 1)], sem_red_send.at[r], sem_red.at[r])
 
     def red_start(r, moments):
-        row = jnp.zeros((SUB, LANES), F32)
-        for m, acc in enumerate(moments):
-            total = jnp.sum(acc, axis=1, keepdims=True)
-            row = row + jnp.where(
-                jnp.logical_and(packed_at, lax.rem(lane, GAP) == m), total, 0.0
-            )
-        packed = jnp.sum(row, axis=0, keepdims=True)
+        packed = jnp.concatenate([jnp.sum(acc, axis=0, keepdims=True) for acc in moments], axis=0)
         red_src[r] = packed
         red_buf[r, s] = packed
         for j in range(1, ns):
@@ -602,21 +592,11 @@
 
     def red_wait(r):
         red_all(r).wait_recv()
-        total = red_buf[r, 0]
-        for j in range(1, ns):
-            total = total + red_buf[r, j]
-        full = jnp.where(packed_at, jnp.broadcast_to(total, (SUB, LANES)), 0.0)
-        out = []
-        for m in range(4):
-            val = jnp.sum(
-                jnp.where(lax.rem(lane, GAP) == m, full, 0.0), axis=1, keepdims=True
-            )
-            val = jnp.broadcast_to(val, (SUB, LANES))
-            both = val
-            for h in range(1, HV):
-                both = both + pltpu.roll(val, ND * h, 0)
-            out.append(both)
-        return out
+        sums = [red_buf[r, j] for j in range(ns)]
+        while len(sums) > 1:
+            sums = [x + y for x, y in zip(sums[::2], sums[1::2])]
+        total = jnp.sum(sums[0], axis=1, keepdims=True)
+        return [jnp.broadcast_to(total[m : m + 1], (SUB, LANES)) for m in range(4)]
 
     def weights(moments):
         m0, m1, m2, m3 = moments
@@ -705,7 +685,7 @@
 
     def begin(q, base):
         mo = first_pass(q, p_ops, f, w, None, PN)
-        halo_pass(q, p_ops, f, w, None, 1, 1)
+        halo_pass(q, p_ops, f, w, None, 1)
         (m3,) = second_pass(q, p_ops, w, None, PN, v)
         red_start(base + q, (*mo, m3))
 
@@ -714,27 +694,27 @@
         def _():
             strip_do(f_strip(q), recv=True)
 
-        halo_pass(q, p_ops, f, w, None, K - 1, K - 2, 1)
-        halo_pass(q, p_ops, w, v, None, 2, 2)
+        halo_pass(q, p_ops, f, w, None, K - 1, 1)
+        halo_pass(q, p_ops, w, v, None, 2)
 
     def displace(q, base):
         y0, y1 = weights(red_wait(base + q))
         save(q, 0, (y0, y1))
 
         def press(i, a):
-            for g in range(2):
-                l = 1 + 2 * i + g
+            for g in range(13):
+                l = 1 + 13 * i + g
                 for y in range(yh):
                     p1[q, l, y] = y0 * f[q, l, y] + y1 * w[q, l, y]
             return a
 
-        lax.fori_loop(0, (LT - 2) // 2, press, 0)
+        lax.fori_loop(0, (LT - 2) // 13, press, 0)
 
         def grad(i, a):
-            l0 = 2 + 4 * i
+            l0 = 2 + 8 * i
             val = Rows(p1, l0, (q,))
             for y in range(yh):
-                for g in range(4):
+                for g in range(8):
                     coef = hb[l0 + g, y]
                     x = val(g, y)
                     b[q, 0, l0 + g, y] = coef * (val(g + 1, y) - val(g - 1, y))
@@ -744,14 +724,14 @@
                     )
             return a
 
-        lax.fori_loop(0, (LT - 4) // 4, grad, 0)
+        lax.fori_loop(0, (LT - 4) // 8, grad, 0)
         mo = first_pass(q, e_ops, b, we, 3, EN)
-        halo_pass(q, e_ops, b, we, 3, 1, 1)
+        halo_pass(q, e_ops, b, we, 3, 1)
         (m3,) = second_pass(q, e_ops, we, 3, EN)
         red_start(base + NB + q, (*mo, m3))
 
     def displace_far(q):
-        halo_pass(q, e_ops, b, we, 3, K - 3, 2, 1)
+        halo_pass(q, e_ops, b, we, 3, K - 3, 1)
 
     def again(q, base, idx):
         z0, z1 = weights(red_wait(base + NB + q))
@@ -779,21 +759,21 @@
                     r2[q, l, y] = f[q, l, y] - div + st[l, y] * p1[q, l, y] - image
             return a
 
-        own_loop(4, resid, 0)
-        halo_loop(2, 2, resid)
+        own_loop(8, resid, 0)
+        both_halos(2, 0, lambda l0, n: resid(l0, n, 0), [(r2, (q,))])
         mo = first_pass(q, p_ops, r2, w2, None, PN)
 
         @pl.when(idx == 0)
         def _():
             strip_do(r_strip(q), start=True)
 
-        halo_pass(q, p_ops, r2, w2, None, 1, 1)
+        halo_pass(q, p_ops, r2, w2, None, 1)
         (m3,) = second_pass(q, p_ops, w2, None, PN)
         red_start(base + 2 * NB + q, (*mo, m3))
 
     def again_far(q):
         strip_do(r_strip(q), recv=True, sent=True)
-        halo_pass(q, p_ops, r2, w2, None, 2, 1, 1)
+        halo_pass(q, p_ops, r2, w2, None, 2, 1)
 
     def close(q, base, idx):
         x0, x1 = weights(red_wait(base + 2 * NB + q))
@@ -804,34 +784,32 @@
         @pl.when(idx == 0)
         def _():
             def update(i, a):
-                for g in range(2):
-                    l = O - NEAR + 2 * i + g
+                for g in range(4):
+                    l = O - NEAR + 4 * i + g
                     for y in range(yh):
                         f[q, l, y] = total(l, y) * row_of(c_obs, l, y)
                 return a
 
-            lax.fori_loop(0, NL // 2 + NEAR, update, 0)
+            lax.fori_loop(0, (NL + 2 * NEAR) // 4, update, 0)
             strip_do(f_strip(q), start=True)
+            begin(q, base + NB * 3)
 
         @pl.when(idx > 0)
         def _():
             def finish(i, a):
-                for g in range(2):
-                    l = 2 * i + g
+                for g in range(4):
+                    l = 4 * i + g
                     for y in range(yh):
                         ybuf[q, l, y] = total(O + l, y) * row_of(c_bs, O + l, y)
                 return a
 
-            lax.fori_loop(0, NL // 2, finish, 0)
+            lax.fori_loop(0, NL // 4, finish, 0)
             for l in range(per):
                 for j in range(1, nq):
                     gram_copy(q, l, lax.rem(me + j, nq), me).start()
 
     def solve(idx, a):
         base = idx * NB * 3
-        with jax.named_scope("g_P1"):
-            each(begin, base)
-
         @pl.when(idx == 0)
         def _():
             far_layers()
@@ -856,6 +834,8 @@
             each(close, base, idx)
         return a
 
+    phase("g_P1")
+    each(begin, 0)
     phase()
     lax.fori_loop(0, 2, solve, 0)
 
@@ -867,10 +847,8 @@
         def layer(i, a):
             for q in range(NB):
                 for y in range(yh):
-                    val = ybuf[q, at + i, y]
-                    for h in range(HV):
-                        row = (q * ND * OWN + i) * ny + h * yh + y
-                        flat[pl.ds(row, ND, stride=OWN * ny), :] = val[h * ND : (h + 1) * ND]
+                    row = (q * OWN + i) * ny + y
+                    flat[pl.ds(row, HV, stride=yh), :] = ybuf[q, at + i, y]
             return a
 
         lax.fori_loop(0, OWN, layer, 0)
@@ -890,8 +868,10 @@
     put.start()
     put_in = pltpu.make_async_copy(hin, hess.at[pl.ds(NDEV * (1 - c), NDEV)], sem_out.at[1])
 
-    width = nq * NB * SUB
-    g_all = jnp.zeros((width, width), F32)
+    ndir = nq * NDEV
+    step = per * yh * SUB
+    gflat = grecv.reshape(ndir * step, LANES)
+    g_all = jnp.zeros((ndir, ndir), F32)
     for l in range(per):
         phase("m_gramwait")
         for q in range(NB):
@@ -900,9 +880,13 @@
             swap.wait_recv()
             put_in.start()
         phase("m_gramdot")
-        for y in range(0, yh, 2):
+        for y in range(yh):
             z = jnp.concatenate(
-                [grecv[:, :, l, y + i].reshape(width, LANES) for i in range(2)], axis=1
+                [
+                    gflat[pl.ds((l * yh + y) * SUB + h, ndir, stride=step), :]
+                    for h in range(SUB)
+                ],
+                axis=1,
             )
             g_all = g_all + lax.dot_general(
                 z,
@@ -911,29 +895,9 @@
                 precision=lax.Precision.HIGHEST,
                 preferred_element_type=F32,
             )
-    phase("m_fold")
-    ndir = nq * NDEV
-    fold = jnp.zeros((ndir, LANES), F32)
-    for h in range(HV):
-        ri = lax.broadcasted_iota(jnp.int32, (ndir, width), 0)
-        ci = lax.broadcasted_iota(jnp.int32, (ndir, width), 1)
-        left_sel = jnp.where(ci == (ri // ND) * SUB + h * ND + lax.rem(ri, ND), 1.0, 0.0)
-        rj = lax.broadcasted_iota(jnp.int32, (width, LANES), 0)
-        cj = lax.broadcasted_iota(jnp.int32, (width, LANES), 1)
-        right_sel = jnp.where(
-            jnp.logical_and(rj == (cj // ND) * SUB + h * ND + lax.rem(cj, ND), cj < ndir),
-            1.0,
-            0.0,
-        )
-        mid = jnp.dot(
-            left_sel, g_all, precision=lax.Precision.HIGHEST, preferred_element_type=F32
-        )
-        fold = fold + jnp.dot(
-            mid, right_sel, precision=lax.Precision.HIGHEST, preferred_element_type=F32
-        )
-    packed = fold[0:SUB]
-    for k in range(1, ndir // SUB):
-        packed = packed + pltpu.roll(fold[k * SUB : (k + 1) * SUB], ndir * k, 1)
+    packed = jnp.concatenate(
+        [g_all[k * SUB : (k + 1) * SUB] for k in range(ndir // SUB)], axis=1
+    )
 
     phase("n_ga")
     ga_src[...] = packed
@@ -1009,8 +973,8 @@
     phase()
 
 
-PN = 4
-EN = 4
+PN = 8
+EN = 8
 
 
 AHEAD = 3
@@ -1104,8 +1068,8 @@
             *[pltpu.VMEM((NDEV, OWN, ny, nz), F32)] * 3,
             pltpu.VMEM((nq, NB, per, yh, SUB, nz), F32),
             pltpu.VMEM((NB, 2, SUB, nz), F32),
-            pltpu.VMEM((NRED, 1, nz), F32),
-            pltpu.VMEM((NRED, ns, 1, nz), F32),
+            pltpu.VMEM((NRED, 4, nz), F32),
+            pltpu.VMEM((NRED, ns, 4, nz), F32),
             pltpu.VMEM((SUB, nz), F32),
             pltpu.VMEM((ns, SUB, nz), F32),
             pltpu.VMEM((SUB, nz), F32),

time: 102 us -> 100 us (0.980)
  Pallas kernels: 101 us -> 98.5 us
    pallas_call x1, Pallas kernels: 97.1 us -> 94.9 us  [body(): pl.pallas_call(functools.partial(kernel, ns, nd, cells), out_shape=(jax.S...]
where the time goes in v4:
time: 100 us; the launch traced here: 99.1 us
  Pallas kernels  98.5 us (98%)
    pallas_call x1, Pallas kernels, body(): pl.pallas_call(functools.partial(kernel, ns, nd, cells), out_shape=(jax.S...  94.9 us
    pallas_call x1, Pallas kernels, body(): pl.pallas_call(last_kernel, out_shape=(jax.ShapeDtypeStruct((ndir, ndir),...  3.56 us

profile of v4, /device:TPU:0, one launch (start us, length us, event | category | flops | bytes accessed | tf_op | source)
XLA Modules:
  0.0 99.1 jit_solution(3892771996165417759)
XLA Ops:
  0.6 94.9 %solve.1 = (f32[8,8,32,128]{3,2,1,0:T(8,128)}, f32[32,128]{1,0:T(8,128)}) custom-call(f32[8,8,32,128]{3,2,1,0:T(8,128)} %probes_at.1, f32[8,32,128]{2,1,0:T(8,128)} %bs_at.1, f32[8,32,128]{2,1,0:T(8,128)} %obs_at.1, f32[8,32,128]{2,1,0:T(8,128)} %perm_at.1, s32[8,32,128]{2,1,0:T(8,128)} %mat_at.1, f32[8]{0:T(128)} %t_storage.1, f32[8]{0:T(128)} %t_alpha.1, ...), custom_call_target="tpu_custom_call" | custom-call | tf_op jit(solution)/shard_map/solve/pallas_call | solution.py:1094
  95.6 3.6 %factor.1 = (f32[32,32]{1,0:T(8,128)}, f32[8,8,32,128]{3,2,1,0:T(8,128)}) custom-call(f32[32,128]{1,0:T(8,128)} %get-tuple-element.6.gram, f32[8,8,32,128]{3,2,1,0:T(8,128)} %get-tuple-element.7.h_in), custom_call_target="tpu_custom_call" | custom-call | tf_op jit(solution)/shard_map/factor/pallas_call | solution.py:1108
